TPU v7x, 32 devices: a whole 2x2x4 slice. The times are simulated.
32 devices in a mesh: dp: 8 (over y, x, core), rep: 4 (over z).
Axes of the slice: x: 2, y: 2, z: 4, core: 2. Of those that a mesh axis runs over, the one named last changes fastest.
Arguments:
- student_in: bfloat16 [16384, 320], P(('dp', 'rep')), may hold values from -6 to 6
- target_in: bfloat16 [16384, 320], P(('dp', 'rep')), may hold values from -6 to 6
- timesteps: int32 [64], P(('dp', 'rep')), may hold values from 20 to 999
- student_win: float32 [1280, 320], P('dp'), may hold values from -0.3125 to 0.3125
- student_wout: float32 [640, 320], P('dp'), may hold values from -0.25 to 0.25
- student_wtime: float32 [640, 320], P('dp'), may hold values from -0.25 to 0.25
- student_gain: float32 [320], replicated, may hold values from 0.5 to 1.5
- student_bias: float32 [320], replicated, may hold values from -3 to 3
- target_win: float32 [1280, 320], P('dp'), may hold values from -0.3125 to 0.3125
- target_wout: float32 [640, 320], P('dp'), may hold values from -0.25 to 0.25
- target_wtime: float32 [640, 320], P('dp'), may hold values from -0.25 to 0.25
- target_gain: float32 [320], replicated, may hold values from 0.5 to 1.5
- target_bias: float32 [320], replicated, may hold values from -3 to 3
Outputs:
- grad_win: float32 [1280, 320], P('dp')
- grad_wout: float32 [640, 320], P('dp')
- grad_wtime: float32 [640, 320], P('dp')
- grad_gain: float32 [320], replicated
- grad_bias: float32 [320], replicated
- ema_win: float32 [1280, 320], P('dp')
- ema_wout: float32 [640, 320], P('dp')
- ema_wtime: float32 [640, 320], P('dp')
- ema_gain: float32 [320], replicated
- ema_bias: float32 [320], replicated
Inputs may be any that keep to these rules, and one draw needn't show every extreme that they name: `timesteps`: student timestep of each sample; the target is evaluated at 20 steps earlier.
All inputs are finite; a program needn't handle non-finite values.
Results may differ from a plain program's by a relative error of at most 0.004.
The roundings to bfloat16 on the way count: a program that leaves them out, or rounds other values in their place, can miss the bound.
Values may be sent and summed in bfloat16 or wider, within the bound.
A program may use at most 64 MiB of HBM per device.

v0:
```python
import functools
import math

import jax
import jax.numpy as jnp
from jax import lax
from jax.experimental import pallas as pl
from jax.experimental.pallas import tpu as pltpu
from jax.sharding import PartitionSpec as P

MESH = pl.DeviceIdType.MESH
SUB = 8

SKIP = 20


ema_decay = 0.95
learn_rate = 0.05


def sinusoid(step_ids, width):
    half_width = width // 2
    frequency = jnp.exp(-math.log(10000.0) * jnp.arange(half_width, dtype=jnp.float32) / half_width)
    angles = step_ids.astype(jnp.float32)[:, None] * frequency[None, :]
    return jnp.concatenate([jnp.cos(angles), jnp.sin(angles)], axis=1)


def gelu_tanh(value):
    inner = 0.7978845608 * (value + 0.044715 * value * value * value)
    return 0.5 * value * (1.0 + jnp.tanh(inner))


def gelu_slope(value):
    tangent = jnp.tanh(0.7978845608 * (value + 0.044715 * value * value * value))
    return 0.5 * (1.0 + tangent) + 0.5 * value * (1.0 - tangent * tangent) * 0.7978845608 * (
        1.0 + 0.134145 * value * value
    )


def contract_last(left, right):
    return lax.dot_general(
        left, right, (((1,), (1,)), ((), ())), preferred_element_type=jnp.float32
    )


def contract_first(left, right):
    return lax.dot_general(
        left, right, (((0,), (0,)), ((), ())), preferred_element_type=jnp.float32
    )


def forward(tok_rows, step_ids, w_in, w_out, w_time, gain, bias):
    time_feat = jax.nn.silu(sinusoid(step_ids, w_time.shape[0])).astype(jnp.bfloat16)
    embedding = jnp.dot(time_feat, w_time, preferred_element_type=jnp.float32)
    samples = step_ids.shape[0]
    width = tok_rows.shape[1]
    summed = tok_rows.astype(jnp.float32).reshape(samples, -1, width) + embedding[:, None, :]
    summed = summed.reshape(-1, width)
    center = summed - jnp.mean(summed, axis=1, keepdims=True)
    inv_std = lax.rsqrt(jnp.mean(center * center, axis=1, keepdims=True) + 1e-05)
    normed = center * inv_std
    normed_b = (normed * gain + bias).astype(jnp.bfloat16)
    mixed = contract_last(normed_b, w_in)
    hidden_count = w_out.shape[0]
    gate_part = mixed[:, :hidden_count]
    up_part = mixed[:, hidden_count:]
    gelu_gate = gelu_tanh(gate_part)
    hidden = (gelu_gate * up_part).astype(jnp.bfloat16)
    output = summed + jnp.dot(hidden, w_out, preferred_element_type=jnp.float32)
    return (output, (time_feat, normed, inv_std, normed_b, gate_part, up_part, gelu_gate, hidden))


def backward(grad_y, saved, w_in, w_out, gain):
    time_feat, normed, inv_std, normed_b, gate_part, up_part, gelu_gate, hidden = saved
    grad_yb = grad_y.astype(jnp.bfloat16)
    grad_h = contract_last(grad_yb, w_out)
    grad_mix = jnp.concatenate(
        [grad_h * up_part * gelu_slope(gate_part), grad_h * gelu_gate], axis=1
    ).astype(jnp.bfloat16)
    grad_z = jnp.dot(grad_mix, w_in, preferred_element_type=jnp.float32)
    grad_gain = jnp.sum(grad_z * normed, axis=0)
    grad_bias = jnp.sum(grad_z, axis=0)
    grad_n = grad_z * gain
    grad_s = grad_y + inv_std * (
        grad_n
        - jnp.mean(grad_n, axis=1, keepdims=True)
        - normed * jnp.mean(grad_n * normed, axis=1, keepdims=True)
    )
    samples = time_feat.shape[0]
    grad_emb = jnp.sum(grad_s.reshape(samples, -1, grad_s.shape[1]), axis=1)
    grad_time = lax.dot_general(
        time_feat.astype(jnp.float32),
        grad_emb,
        (((0,), (0,)), ((), ())),
        precision=lax.Precision.HIGHEST,
        preferred_element_type=jnp.float32,
    )
    return (grad_yb, grad_mix, grad_gain, grad_bias, grad_time)


def fetch(piece_in, piece_out, piece_time):
    return (
        lax.all_gather(piece_in, "dp", axis=0, tiled=True),
        lax.all_gather(piece_out, "dp", axis=0, tiled=True),
        lax.all_gather(piece_time, "dp", axis=0, tiled=True),
    )


def per_device(
    student_in,
    target_in,
    timesteps,
    student_win,
    student_wout,
    student_wtime,
    student_gain,
    student_bias,
    target_win,
    target_wout,
    target_wtime,
    target_gain,
    target_bias,
):
    s_in, s_out, s_time = fetch(
        student_win.astype(jnp.bfloat16),
        student_wout.astype(jnp.bfloat16),
        student_wtime.astype(jnp.bfloat16),
    )
    student_out, saved = forward(
        student_in, timesteps, s_in, s_out, s_time, student_gain, student_bias
    )
    t_in, t_out, t_time = fetch(
        target_win.astype(jnp.bfloat16),
        target_wout.astype(jnp.bfloat16),
        target_wtime.astype(jnp.bfloat16),
    )
    target_out, unused = forward(
        target_in, timesteps - SKIP, t_in, t_out, t_time, target_gain, target_bias
    )
    grad_y = (student_out - target_out) / student_in.shape[0]
    back_in, back_out = (
        lax.all_gather(student_win.astype(jnp.bfloat16), "dp", axis=0, tiled=True),
        lax.all_gather(student_wout.astype(jnp.bfloat16), "dp", axis=0, tiled=True),
    )
    grad_yb, grad_mix, grad_gain, grad_bias, grad_time = backward(
        grad_y, saved, back_in, back_out, student_gain
    )
    normed_b = saved[3]
    hidden = saved[7]
    part = grad_mix
    shard_in = lax.psum_scatter(
        contract_first(part, normed_b), "dp", scatter_dimension=0, tiled=True
    )
    part = hidden
    shard_out = lax.psum_scatter(
        contract_first(part, grad_yb), "dp", scatter_dimension=0, tiled=True
    )
    shard_time = lax.psum_scatter(grad_time, "dp", scatter_dimension=0, tiled=True)
    shard_in, shard_out, shard_time = lax.psum((shard_in, shard_out, shard_time), "rep")
    total_gain, total_bias = lax.psum((grad_gain, grad_bias), ("dp", "rep"))

    def average(target_p, student_p, grad_p):
        return ema_decay * target_p + (1.0 - ema_decay) * (student_p - learn_rate * grad_p)

    return (
        shard_in,
        shard_out,
        shard_time,
        total_gain,
        total_bias,
        average(target_win, student_win, shard_in),
        average(target_wout, student_wout, shard_out),
        average(target_wtime, student_wtime, shard_time),
        average(target_gain, student_gain, total_gain),
        average(target_bias, student_bias, total_bias),
    )


def time_features(step_ids, width):
    return jax.nn.silu(sinusoid(step_ids, width)).astype(jnp.bfloat16)


def fused_kernel(
    n_rep, n_sam,
    x_s, x_t, tf, sw, so, st, sg, sb, tw, to, tt, tg, tb,
    fin_o, sum_o,
    ws_all, os_all, wt_all, ot_all,
    tf_all, e_part, e_in, small, small_rep,
    normed_v, inv_v, nb_v, hid_v, a_v, b_v, y_v, nbt_v, gyb_v, gma_v, gmb_v,
    g_win, g_out, gb_win, gb_out, r1_win, r1_out, s2_win, s2_out, r2_win, r2_out,
    p_v, pb_v, r3_v, fin_v,
    g_send, g_recv, tf_send, tf_recv, e_send, e_recv, sm_send, sm_recv,
    r1_send, r1_recv, r2_send, r2_recv, r3_send, r3_recv, r4_send, r4_recv, rs_send, rs_recv,
):
    f32, bf16 = jnp.float32, jnp.bfloat16
    me, rep = lax.axis_index("dp"), lax.axis_index("rep")
    core, col, row = lax.rem(me, 2), lax.rem(lax.div(me, 2), 2), lax.div(me, 4)
    rows_in, rows_out, rows_time = sw.shape[0], so.shape[0], st.shape[0]
    tokens, width = x_s.shape[1], x_s.shape[0]
    per = tokens // n_sam
    ff = os_all.shape[0]

    def peer(t):
        flip = lambda b, on: 1 - b if on else b
        return flip(row, t & 4) * 4 + flip(col, t & 2) * 2 + flip(core, t & 1)

    def dp_id(t):
        return {"dp": peer(t)}

    def rep_at(j):
        return lax.rem(rep + j, n_rep)

    sends = []

    def send(src, dst, s_sem, r_sem, where):
        copy = pltpu.make_async_remote_copy(
            src_ref=src, dst_ref=dst, send_sem=s_sem, recv_sem=r_sem,
            device_id=where, device_id_type=MESH,
        )
        copy.start()
        sends.append(copy)

    def arrive(dst, s_sem, r_sem):
        pltpu.make_async_remote_copy(
            src_ref=dst, dst_ref=dst, send_sem=s_sem, recv_sem=r_sem,
            device_id=dp_id(1), device_id_type=MESH,
        ).wait_recv()

    def block(ref, owner, count):
        return ref.at[pl.ds(pl.multiple_of(owner * count, 16), count)]

    bufs = (ws_all, os_all, wt_all, ot_all)
    counts = (rows_in, rows_out, rows_in, rows_out)
    firsts = (2, 4, 4, 2)
    for buf, own, count in zip(bufs, (sw, so, tw, to), counts):
        buf[pl.ds(pl.multiple_of(me * count, 16), count), :] = own[...].astype(bf16)
    tf_all[pl.ds(me, 1)] = tf[pl.ds(me, 1)]

    barrier = pltpu.get_barrier_semaphore()
    for t in range(1, 8):
        pl.semaphore_signal(barrier, inc=1, device_id=dp_id(t), device_id_type=MESH)
    for j in range(1, n_rep):
        pl.semaphore_signal(barrier, inc=1, device_id={"rep": rep_at(j)}, device_id_type=MESH)
    pl.semaphore_wait(barrier, 7 + n_rep - 1)

    def push(seg, orel, t, k):
        part = block(bufs[seg], peer(orel), counts[seg])
        send(part, part, g_send.at[seg * 8 + k], g_recv.at[seg * 8 + (orel ^ t)], dp_id(t))

    def landed(seg, orel):
        arrive(block(bufs[seg], peer(orel), counts[seg]), g_send.at[0], g_recv.at[seg * 8 + orel])

    def open_gather(seg):
        push(seg, 0, firsts[seg], 0)
        push(seg, 0, 6 - firsts[seg], 1)
        push(seg, 0, 1, 2)

    def relay_near(seg):
        first, second = firsts[seg], 6 - firsts[seg]
        landed(seg, first)
        push(seg, first, second, 3)
        push(seg, first, 1, 4)
        landed(seg, second)
        push(seg, second, 1, 5)

    def relay_far(seg):
        landed(seg, 6)
        push(seg, 6, 1, 6)

    def close_gather(seg):
        for orel in (1, 3, 5, 7):
            landed(seg, orel)

    for t in range(1, 8):
        send(tf.at[peer(t)], tf_all.at[me], tf_send.at[t], tf_recv.at[t], dp_id(t))
    open_gather(0)
    for t in range(1, 8):
        arrive(tf_all.at[peer(t)], tf_send.at[t], tf_recv.at[t])
    feats = tf_all[...].reshape(8 * SUB, rows_time).astype(bf16)
    part_s = jnp.dot(feats, st[...].astype(bf16), preferred_element_type=f32)
    part_t = jnp.dot(feats, tt[...].astype(bf16), preferred_element_type=f32)
    line = lax.rem(lax.broadcasted_iota(jnp.int32, part_s.shape, 0), SUB)
    e_part[...] = jnp.where(line < n_sam, part_s, part_t).reshape(e_part.shape)
    e_in[pl.ds(me, 1)] = e_part[pl.ds(me, 1)]
    for t in range(1, 8):
        send(e_part.at[peer(t)], e_in.at[me], e_send.at[t], e_recv.at[t], dp_id(t))
    open_gather(1)
    open_gather(2)
    open_gather(3)
    relay_near(0)
    for t in range(1, 8):
        arrive(e_in.at[peer(t)], e_send.at[t], e_recv.at[t])
    emb = e_in[0]
    for k in range(1, 8):
        emb = emb + e_in[k]

    def normalise(x_ref, k, shift, gain, bias):
        summed = x_ref[:, pl.ds(k * per, per)].astype(f32).T + shift
        center = summed - jnp.mean(summed, axis=1, keepdims=True)
        inv = lax.rsqrt(jnp.mean(center * center, axis=1, keepdims=True) + 1e-05)
        normed = center * inv
        return summed, inv, normed, (normed * gain + bias).astype(bf16)

    for k in range(n_sam):
        at = pl.ds(k * per, per)
        summed, inv, normed, nb = normalise(x_s, k, emb[k : k + 1], sg[...][None], sb[...][None])
        y_v[at, :], normed_v[at, :], nb_v[at, :] = summed, normed, nb
        inv_v[at, :] = inv
    relay_far(0)
    relay_near(1)
    for k in range(n_sam):
        at = pl.ds(k * per, per)
        summed, inv, normed, nb = normalise(x_t, k, emb[n_sam + k : n_sam + k + 1], tg[...][None], tb[...][None])
        y_v[at, :], nbt_v[at, :] = y_v[at, :] - summed, nb
    close_gather(0)
    relay_far(1)

    for k in range(n_sam):
        at = pl.ds(k * per, per)
        gate = contract_last(nb_v[at, :], ws_all[:ff, :])
        up = contract_last(nb_v[at, :], ws_all[ff:, :])
        tangent = jnp.tanh(0.7978845608 * (gate + 0.044715 * gate * gate * gate))
        half = 0.5 * (1.0 + tangent)
        act = gate * half
        slope = half + 0.5 * gate * (1.0 - tangent * tangent) * 0.7978845608 * (
            1.0 + 0.134145 * gate * gate
        )
        a_v[at, :], b_v[at, :] = up * slope, act
        hid_v[at, :] = (act * up).astype(bf16)
        if k == 0:
            relay_near(2)
            close_gather(1)
    relay_far(2)
    relay_near(3)
    for k in range(n_sam):
        at = pl.ds(k * per, per)
        y_v[at, :] = y_v[at, :] + jnp.dot(hid_v[at, :], os_all[...], preferred_element_type=f32)
    close_gather(2)
    relay_far(3)

    for k in range(n_sam):
        at = pl.ds(k * per, per)
        gate = contract_last(nbt_v[at, :], wt_all[:ff, :])
        up = contract_last(nbt_v[at, :], wt_all[ff:, :])
        hid = (gelu_tanh(gate) * up).astype(bf16)
        if k == 0:
            close_gather(3)
        gy = (y_v[at, :] - jnp.dot(hid, ot_all[...], preferred_element_type=f32)) * (1.0 / tokens)
        y_v[at, :], gyb_v[at, :] = gy, gy.astype(bf16)

    total_out = contract_first(hid_v[...], gyb_v[...])
    g_out[...], gb_out[...] = total_out, total_out.astype(bf16)

    def to_core(src, dst, count, q, k):
        send(block(src, 2 * q + 1 - core, count), dst.at[q], r1_send.at[k], r1_recv.at[k], dp_id(1))

    for q in range(4):
        to_core(gb_out, r1_out, rows_out, q, q)

    grad_gain = jnp.zeros((1, width), f32)
    grad_bias = grad_gain
    embs = []
    for k in range(n_sam):
        at = pl.ds(k * per, per)
        gh = contract_last(gyb_v[at, :], os_all[...])
        gma, gmb = (gh * a_v[at, :]).astype(bf16), (gh * b_v[at, :]).astype(bf16)
        gma_v[at, :], gmb_v[at, :] = gma, gmb
        gz = jnp.dot(gma, ws_all[:ff, :], preferred_element_type=f32) + jnp.dot(
            gmb, ws_all[ff:, :], preferred_element_type=f32
        )
        normed = normed_v[at, :]
        grad_gain = grad_gain + jnp.sum(gz * normed, axis=0, keepdims=True)
        grad_bias = grad_bias + jnp.sum(gz, axis=0, keepdims=True)
        gn = gz * sg[...][None]
        gs = y_v[at, :] + inv_v[at, :] * (
            gn
            - jnp.mean(gn, axis=1, keepdims=True)
            - normed * jnp.mean(gn * normed, axis=1, keepdims=True)
        )
        embs.append(jnp.sum(gs, axis=0, keepdims=True))
    fill = jnp.zeros((SUB - n_sam - 2, width), f32)
    small[pl.ds(me, 1)] = jnp.concatenate(embs + [grad_gain, grad_bias, fill], axis=0)[None]

    for h, gm in enumerate((gma_v, gmb_v)):
        total = contract_first(gm[...], nb_v[...])
        at = pl.ds(h * ff, ff)
        g_win[at, :], gb_win[at, :] = total, total.astype(bf16)
        for q in (2 * h, 2 * h + 1):
            to_core(gb_win, r1_win, rows_in, q, 4 + q)
        if h == 0:
            for t in range(1, 8):
                send(small.at[me], small.at[me], sm_send.at[t], sm_recv.at[t], dp_id(t))

    def pair(g, r1, owner_rel, count):
        owner = peer(owner_rel)
        own = g[pl.ds(pl.multiple_of(owner * count, 16), count), :]
        return own + r1[lax.div(owner, 2)].astype(f32)

    for g, r1, s2, r2, count, base in (
        (g_out, r1_out, s2_out, r2_out, rows_out, 0),
        (g_win, r1_win, s2_win, r2_win, rows_in, 4),
    ):
        for q in range(4):
            arrive(r1.at[q], r1_send.at[base + q], r1_recv.at[base + q])
        for k in (3, 1, 2):
            s2[k] = pair(g, r1, 2 * k, count).astype(bf16)
            send(s2.at[k], r2.at[k], r2_send.at[base + k], r2_recv.at[base + k], dp_id(2 * k))

    for t in range(1, 8):
        arrive(small.at[peer(t)], sm_send.at[t], sm_recv.at[t])
    feats = tf_all[...].reshape(8 * SUB, rows_time)
    line = lax.rem(lax.broadcasted_iota(jnp.int32, feats.shape, 0), SUB)
    feats = jnp.where(line < n_sam, feats, 0.0)
    p_v[pl.ds(rows_in + rows_out, rows_time), :] = lax.dot_general(
        feats,
        small[...].reshape(8 * SUB, width),
        (((0,), (0,)), ((), ())),
        precision=lax.Precision.HIGHEST,
        preferred_element_type=f32,
    )
    sums = small[0]
    for k in range(1, 8):
        sums = sums + small[k]
    small_rep[pl.ds(rep, 1)] = sums[None]
    for j in range(1, n_rep):
        send(small_rep.at[rep], small_rep.at[rep], rs_send.at[j], rs_recv.at[j], {"rep": rep_at(j)})

    for g, r1, r2, count, base, start in (
        (g_out, r1_out, r2_out, rows_out, 0, rows_in),
        (g_win, r1_win, r2_win, rows_in, 4, 0),
    ):
        total = pair(g, r1, 0, count)
        for k in (1, 2, 3):
            arrive(r2.at[k], r2_send.at[base + k], r2_recv.at[base + k])
            total = total + r2[k].astype(f32)
        p_v[pl.ds(start, count), :] = total
    pb_v[...] = p_v[...].astype(bf16)

    share = p_v.shape[0] // n_rep
    for j in range(1, n_rep):
        send(block(pb_v, rep_at(j), share), r3_v.at[j], r3_send.at[j], r3_recv.at[j], {"rep": rep_at(j)})
    mine = pl.ds(pl.multiple_of(rep * share, 16), share)
    total = p_v[mine, :]
    for j in range(1, n_rep):
        arrive(r3_v.at[j], r3_send.at[j], r3_recv.at[j])
        total = total + r3_v[j].astype(f32)
    fin_v[mine, :] = total.astype(bf16)
    for j in range(1, n_rep):
        part = block(fin_v, rep, share)
        send(part, part, r4_send.at[j], r4_recv.at[j], {"rep": rep_at(j)})

    for j in range(1, n_rep):
        arrive(small_rep.at[rep_at(n_rep - j)], rs_send.at[j], rs_recv.at[j])
    sums = small_rep[0]
    for j in range(1, n_rep):
        sums = sums + small_rep[j]

    sum_o[...] = sums
    for j in range(1, n_rep):
        arrive(block(fin_v, rep_at(n_rep - j), share), r4_send.at[j], r4_recv.at[j])
    fin_o[...] = fin_v[...]
    for copy in sends:
        copy.wait_send()


def average(target_p, student_p, grad_p):
    return ema_decay * target_p + (1.0 - ema_decay) * (student_p - learn_rate * grad_p)


def update_kernel(
    n_sam, fin, sums, sw, so, st, sg, sb, tw, to, tt, tg, tb,
    gw_o, go_o, gt_o, gg_o, gb_o, ew_o, eo_o, et_o, eg_o, eb_o,
):
    start = 0
    for g_o, e_o, student, target in (
        (gw_o, ew_o, sw, tw), (go_o, eo_o, so, to), (gt_o, et_o, st, tt),
    ):
        grad = fin[pl.ds(start, g_o.shape[0]), :].astype(jnp.float32)
        g_o[...] = grad
        e_o[...] = average(target[...], student[...], grad)
        start += g_o.shape[0]
    gg, gb = sums[n_sam, :], sums[n_sam + 1, :]
    gg_o[...], gb_o[...] = gg, gb
    eg_o[...] = average(tg[...], sg[...], gg)
    eb_o[...] = average(tb[...], sb[...], gb)


def fused_device(n_dp, n_rep, *args):
    (student_in, target_in, timesteps, sw, so, st, sg, sb, tw, to, tt, tg, tb) = args
    f32, bf16 = jnp.float32, jnp.bfloat16
    tokens, width = student_in.shape
    n_sam = timesteps.shape[0]
    rows_in, rows_out, rows_time = sw.shape[0], so.shape[0], st.shape[0]
    ff = rows_out * n_dp
    both = jnp.concatenate([timesteps, timesteps - SKIP])
    feats = time_features(both, rows_time * n_dp).astype(f32)
    feats = jnp.pad(feats, ((0, SUB - 2 * n_sam), (0, 0)))
    feats = feats.reshape(SUB, n_dp, rows_time).transpose(1, 0, 2)
    rows_all = rows_in + rows_out + rows_time
    vm = pltpu.VMEM
    dma = pltpu.SemaphoreType.DMA
    scratch = [
        vm((n_dp * rows_in, width), bf16), vm((ff, width), bf16),
        vm((n_dp * rows_in, width), bf16), vm((ff, width), bf16),
        vm((n_dp, SUB, rows_time), f32), vm((n_dp, SUB, width), f32), vm((n_dp, SUB, width), f32),
        vm((n_dp, SUB, width), f32), vm((n_rep, SUB, width), f32),
        vm((tokens, width), f32), vm((tokens, 1), f32), vm((tokens, width), bf16),
        vm((tokens, ff), bf16), vm((tokens, ff), f32), vm((tokens, ff), f32),
        vm((tokens, width), f32), vm((tokens, width), bf16), vm((tokens, width), bf16),
        vm((tokens, ff), bf16), vm((tokens, ff), bf16),
        vm((n_dp * rows_in, width), f32), vm((ff, width), f32),
        vm((n_dp * rows_in, width), bf16), vm((ff, width), bf16),
        vm((4, rows_in, width), bf16), vm((4, rows_out, width), bf16),
        vm((4, rows_in, width), bf16), vm((4, rows_out, width), bf16),
        vm((4, rows_in, width), bf16), vm((4, rows_out, width), bf16),
        vm((rows_all, width), f32), vm((rows_all, width), bf16),
        vm((n_rep, rows_all // n_rep, width), bf16), vm((rows_all, width), bf16),
        dma((32,)), dma((32,)), dma((8,)), dma((8,)), dma((8,)), dma((8,)), dma((8,)), dma((8,)),
        dma((8,)), dma((8,)), dma((8,)), dma((8,)),
        dma((n_rep,)), dma((n_rep,)), dma((n_rep,)), dma((n_rep,)), dma((n_rep,)), dma((n_rep,)),
    ]
    big = [jax.ShapeDtypeStruct(w.shape, f32) for w in (sw, so, st)]
    flat = [jax.ShapeDtypeStruct((width,), f32)] * 2
    fin, sums = pl.pallas_call(
        functools.partial(fused_kernel, n_rep, n_sam),
        out_shape=(
            jax.ShapeDtypeStruct((rows_all, width), bf16),
            jax.ShapeDtypeStruct((SUB, width), f32),
        ),
        in_specs=[pl.BlockSpec(memory_space=vm)] * 13,
        out_specs=[pl.BlockSpec(memory_space=vm)] * 2,
        scratch_shapes=scratch,
        compiler_params=pltpu.CompilerParams(
            collective_id=0, has_side_effects=True, vmem_limit_bytes=56 * 1024 * 1024
        ),
        name="distill_step",
    )(student_in.T, target_in.T, feats, sw, so, st, sg, sb, tw, to, tt, tg, tb)
    return tuple(
        pl.pallas_call(
            functools.partial(update_kernel, n_sam),
            out_shape=(*big, *flat, *big, *flat),
            in_specs=[pl.BlockSpec(memory_space=vm)] * 12,
            out_specs=[pl.BlockSpec(memory_space=vm)] * 10,
            name="average_step",
        )(fin, sums, sw, so, st, sg, sb, tw, to, tt, tg, tb)
    )


def fits_fused(n_dp, n_rep, args):
    tokens, samples = args[0].shape[0], args[2].shape[0]
    n_dev = n_dp * n_rep
    rows = [args[i].shape[0] for i in (3, 4, 5)]
    return (
        n_dp == 8
        and n_rep > 1
        and samples % n_dev == 0
        and 2 * (samples // n_dev) + 0 <= SUB
        and samples // n_dev + 2 <= SUB
        and tokens % samples == 0
        and (tokens // samples) % 128 == 0
        and all(r % (16 * n_dp) == 0 for r in rows)
        and (sum(rows) // n_dp) % (16 * n_rep) == 0
        and rows[0] == 2 * rows[1]
    )


def solution(mesh):
    in_specs = (
        P(("dp", "rep"), None),
        P(("dp", "rep"), None),
        P(("dp", "rep")),
        P("dp", None),
        P("dp", None),
        P("dp", None),
        P(),
        P(),
        P("dp", None),
        P("dp", None),
        P("dp", None),
        P(),
        P(),
    )
    out_specs = (
        P("dp", None),
        P("dp", None),
        P("dp", None),
        P(),
        P(),
        P("dp", None),
        P("dp", None),
        P("dp", None),
        P(),
        P(),
    )
    n_dp, n_rep = mesh.shape["dp"], mesh.shape["rep"]

    def step(*args):
        fused = fits_fused(n_dp, n_rep, args)
        body = functools.partial(fused_device, n_dp, n_rep) if fused else per_device
        return jax.shard_map(
            body, mesh=mesh, in_specs=in_specs, out_specs=out_specs, check_vma=False
        )(*args)

    return step
```

profile of v0, /device:TPU:0, one launch (start us, length us, event | category | flops | bytes accessed | tf_op | source)
XLA Modules:
  0.0 66.9 jit_solution(5037956324792638618)
XLA Ops:
  0.6 0.0 copy-start
  0.7 0.6 copy-done
  1.3 0.1 add_convert_fusion
  1.4 0.1 multiply_cosine_fusion
  1.5 0.1 fusion
  1.6 0.1 reshape.45
  1.7 0.6 copy.25
  2.3 62.1 %distill_step.1 = (bf16[320,320]{1,0:T(8,128)(2,1)}, f32[8,320]{1,0:T(8,128)}) custom-call(bf16[320,512]{1,0:T(8,128)(2,1)} %bitcast.5, bf16[320,512]{1,0:T(8,128)(2,1)} %bitcast.6, f32[8,8,80]{2,1,0:T(8,128)} %bitcast.7, f32[160,320]{1,0:T(8,128)} %sw.3, f32[80,320]{1,0:T(8,128)} %so.3, f32[80,320]{1,0:T(8,128)} %st.3, f32[320]{0:T(512)} %sg.3, f32[320]{0:T(512)} %sb.3, ...), custom_call_target="tpu_custom_call" | custom-call | tf_op jit(solution)/shard_map/distill_step/pallas_call | solution.py:524
  64.4 2.5 %average_step.1 = (f32[160,320]{1,0:T(8,128)}, f32[80,320]{1,0:T(8,128)}, f32[80,320]{1,0:T(8,128)}, f32[320]{0:T(512)}, f32[320]{0:T(512)}, /*index=5*/f32[160,...) custom-call(bf16[320,320]{1,0:T(8,128)(2,1)} %get-tuple-element.12.fin, ...), custom_call_target="tpu_custom_call" | custom-call | tf_op jit(solution)/shard_map/average_step/pallas_call | solution.py:539
  (3 shorter events, 0.0 us)
Async XLA Ops:
  0.6 0.7 copy-start
where the time goes:
time: 67.1 us; the launch traced here: 66.9 us
  Pallas kernels  64.5 us (96%)
  local copies, waits for them, and re-layouts  1.35 us (2%)
  between operations  0.68 us (1%)
    pallas_call x1, Pallas kernels, fused_device(): pl.pallas_call(functools.partial(fused_kernel, n_rep, n_sam), out_shape=(...  62.1 us
    pallas_call x1, Pallas kernels, fused_device(): pl.pallas_call(functools.partial(update_kernel, n_sam), out_shape=(*big,...  2.49 us

commit v1 on v0

v1 whole, which is shorter than its diff:
```python
import functools
import math

import jax
import jax.numpy as jnp
from jax import lax
from jax.experimental import pallas as pl
from jax.experimental.pallas import tpu as pltpu
from jax.sharding import PartitionSpec as P

MESH = pl.DeviceIdType.MESH
SUB = 8

SKIP = 20


ema_decay = 0.95
learn_rate = 0.05


def sinusoid(step_ids, width):
    half_width = width // 2
    frequency = jnp.exp(-math.log(10000.0) * jnp.arange(half_width, dtype=jnp.float32) / half_width)
    angles = step_ids.astype(jnp.float32)[:, None] * frequency[None, :]
    return jnp.concatenate([jnp.cos(angles), jnp.sin(angles)], axis=1)


def gelu_tanh(value):
    inner = 0.7978845608 * (value + 0.044715 * value * value * value)
    return 0.5 * value * (1.0 + jnp.tanh(inner))


def gelu_slope(value):
    tangent = jnp.tanh(0.7978845608 * (value + 0.044715 * value * value * value))
    return 0.5 * (1.0 + tangent) + 0.5 * value * (1.0 - tangent * tangent) * 0.7978845608 * (
        1.0 + 0.134145 * value * value
    )


def contract_last(left, right):
    return lax.dot_general(
        left, right, (((1,), (1,)), ((), ())), preferred_element_type=jnp.float32
    )


def contract_first(left, right):
    return lax.dot_general(
        left, right, (((0,), (0,)), ((), ())), preferred_element_type=jnp.float32
    )


def forward(tok_rows, step_ids, w_in, w_out, w_time, gain, bias):
    time_feat = jax.nn.silu(sinusoid(step_ids, w_time.shape[0])).astype(jnp.bfloat16)
    embedding = jnp.dot(time_feat, w_time, preferred_element_type=jnp.float32)
    samples = step_ids.shape[0]
    width = tok_rows.shape[1]
    summed = tok_rows.astype(jnp.float32).reshape(samples, -1, width) + embedding[:, None, :]
    summed = summed.reshape(-1, width)
    center = summed - jnp.mean(summed, axis=1, keepdims=True)
    inv_std = lax.rsqrt(jnp.mean(center * center, axis=1, keepdims=True) + 1e-05)
    normed = center * inv_std
    normed_b = (normed * gain + bias).astype(jnp.bfloat16)
    mixed = contract_last(normed_b, w_in)
    hidden_count = w_out.shape[0]
    gate_part = mixed[:, :hidden_count]
    up_part = mixed[:, hidden_count:]
    gelu_gate = gelu_tanh(gate_part)
    hidden = (gelu_gate * up_part).astype(jnp.bfloat16)
    output = summed + jnp.dot(hidden, w_out, preferred_element_type=jnp.float32)
    return (output, (time_feat, normed, inv_std, normed_b, gate_part, up_part, gelu_gate, hidden))


def backward(grad_y, saved, w_in, w_out, gain):
    time_feat, normed, inv_std, normed_b, gate_part, up_part, gelu_gate, hidden = saved
    grad_yb = grad_y.astype(jnp.bfloat16)
    grad_h = contract_last(grad_yb, w_out)
    grad_mix = jnp.concatenate(
        [grad_h * up_part * gelu_slope(gate_part), grad_h * gelu_gate], axis=1
    ).astype(jnp.bfloat16)
    grad_z = jnp.dot(grad_mix, w_in, preferred_element_type=jnp.float32)
    grad_gain = jnp.sum(grad_z * normed, axis=0)
    grad_bias = jnp.sum(grad_z, axis=0)
    grad_n = grad_z * gain
    grad_s = grad_y + inv_std * (
        grad_n
        - jnp.mean(grad_n, axis=1, keepdims=True)
        - normed * jnp.mean(grad_n * normed, axis=1, keepdims=True)
    )
    samples = time_feat.shape[0]
    grad_emb = jnp.sum(grad_s.reshape(samples, -1, grad_s.shape[1]), axis=1)
    grad_time = lax.dot_general(
        time_feat.astype(jnp.float32),
        grad_emb,
        (((0,), (0,)), ((), ())),
        precision=lax.Precision.HIGHEST,
        preferred_element_type=jnp.float32,
    )
    return (grad_yb, grad_mix, grad_gain, grad_bias, grad_time)


def fetch(piece_in, piece_out, piece_time):
    return (
        lax.all_gather(piece_in, "dp", axis=0, tiled=True),
        lax.all_gather(piece_out, "dp", axis=0, tiled=True),
        lax.all_gather(piece_time, "dp", axis=0, tiled=True),
    )


def per_device(
    student_in,
    target_in,
    timesteps,
    student_win,
    student_wout,
    student_wtime,
    student_gain,
    student_bias,
    target_win,
    target_wout,
    target_wtime,
    target_gain,
    target_bias,
):
    s_in, s_out, s_time = fetch(
        student_win.astype(jnp.bfloat16),
        student_wout.astype(jnp.bfloat16),
        student_wtime.astype(jnp.bfloat16),
    )
    student_out, saved = forward(
        student_in, timesteps, s_in, s_out, s_time, student_gain, student_bias
    )
    t_in, t_out, t_time = fetch(
        target_win.astype(jnp.bfloat16),
        target_wout.astype(jnp.bfloat16),
        target_wtime.astype(jnp.bfloat16),
    )
    target_out, unused = forward(
        target_in, timesteps - SKIP, t_in, t_out, t_time, target_gain, target_bias
    )
    grad_y = (student_out - target_out) / student_in.shape[0]
    back_in, back_out = (
        lax.all_gather(student_win.astype(jnp.bfloat16), "dp", axis=0, tiled=True),
        lax.all_gather(student_wout.astype(jnp.bfloat16), "dp", axis=0, tiled=True),
    )
    grad_yb, grad_mix, grad_gain, grad_bias, grad_time = backward(
        grad_y, saved, back_in, back_out, student_gain
    )
    normed_b = saved[3]
    hidden = saved[7]
    part = grad_mix
    shard_in = lax.psum_scatter(
        contract_first(part, normed_b), "dp", scatter_dimension=0, tiled=True
    )
    part = hidden
    shard_out = lax.psum_scatter(
        contract_first(part, grad_yb), "dp", scatter_dimension=0, tiled=True
    )
    shard_time = lax.psum_scatter(grad_time, "dp", scatter_dimension=0, tiled=True)
    shard_in, shard_out, shard_time = lax.psum((shard_in, shard_out, shard_time), "rep")
    total_gain, total_bias = lax.psum((grad_gain, grad_bias), ("dp", "rep"))

    def average(target_p, student_p, grad_p):
        return ema_decay * target_p + (1.0 - ema_decay) * (student_p - learn_rate * grad_p)

    return (
        shard_in,
        shard_out,
        shard_time,
        total_gain,
        total_bias,
        average(target_win, student_win, shard_in),
        average(target_wout, student_wout, shard_out),
        average(target_wtime, student_wtime, shard_time),
        average(target_gain, student_gain, total_gain),
        average(target_bias, student_bias, total_bias),
    )


GATE_C = 0.7978845608


def put_packed(ref, value):
    rows, lo = value.shape[0], value.shape[1] // 128 * 128
    for i in range(lo // 128):
        ref[i * rows : (i + 1) * rows, :] = value[:, i * 128 : (i + 1) * 128].astype(ref.dtype)
    at, half = lo // 128 * rows, rows // 2
    rest = jnp.concatenate([value[:half, lo:], value[half:, lo:]], axis=1)
    ref[at : at + half, :] = rest.astype(ref.dtype)


def unpacked(value, rows, width):
    lo = width // 128 * 128
    at, half, rest = lo // 128 * rows, rows // 2, width - lo
    parts = [value[i * rows : (i + 1) * rows] for i in range(lo // 128)]
    tail = value[at : at + half]
    parts.append(jnp.concatenate([tail[:, :rest], tail[:, rest:]], axis=0))
    return jnp.concatenate(parts, axis=1)


def fused_kernel(n_rep, n_sam, names, *refs):
    r = dict(zip(names, refs))
    f32, bf16 = jnp.float32, jnp.bfloat16
    me, rep = lax.axis_index("dp"), lax.axis_index("rep")
    core, col, row = lax.rem(me, 2), lax.rem(lax.div(me, 2), 2), lax.div(me, 4)
    sw, so, st, tw, to, tt = (r[k] for k in ("sw", "so", "st", "tw", "to", "tt"))
    sg, sb, tg, tb, x_s, x_t = (r[k] for k in ("sg", "sb", "tg", "tb", "x_s", "x_t"))
    rows_in, rows_out, rows_time = sw.shape[0], so.shape[0], st.shape[0]
    width, tokens = x_s.shape
    per = tokens // n_sam
    lo = width // 128 * 128
    rest = width - lo
    ws_all, os_all, wt_all, ot_all = (r[k] for k in ("ws_all", "os_all", "wt_all", "ot_all"))
    ff = os_all.shape[0]
    tf_own, tf_all, e_part, e_in = (r[k] for k in ("tf_own", "tf_all", "e_part", "e_in"))
    g_all, e_all = r["g_o"], r["e_o"]

    flip = lambda b, on: 1 - b if on else b

    def peer(t):
        return flip(row, t & 4) * 4 + flip(col, t & 2) * 2 + flip(core, t & 1)

    def dp_id(t):
        return {"dp": peer(t)}

    def rep_peer(j):
        return flip(lax.div(rep, 2), j & 2) * 2 + flip(lax.rem(rep, 2), j & 1)

    def rep_id(j):
        return {"rep": rep_peer(j)}

    barrier = pltpu.get_barrier_semaphore()
    for t in range(1, 8):
        pl.semaphore_signal(barrier, inc=1, device_id=dp_id(t), device_id_type=MESH)
    for j in range(1, n_rep):
        pl.semaphore_signal(barrier, inc=1, device_id=rep_id(j), device_id_type=MESH)

    loads = []
    for i, name in enumerate(LOADED):
        copy = pltpu.make_async_copy(r[name + "_h"], r[name], r["ld_sem"].at[i])
        copy.start()
        loads.append(copy)

    def loaded(*keys):
        for key in keys:
            loads[LOADED.index(key)].wait()

    def send(src, dst, s_sem, r_sem, where):
        pltpu.make_async_remote_copy(
            src_ref=src, dst_ref=dst, send_sem=s_sem, recv_sem=r_sem,
            device_id=where, device_id_type=MESH,
        ).start()

    def bytes_of(ref, sem):
        return pltpu.make_async_remote_copy(
            src_ref=ref, dst_ref=ref, send_sem=sem, recv_sem=sem,
            device_id=dp_id(1), device_id_type=MESH,
        )

    def arrive(ref, sem):
        bytes_of(ref, sem).wait_recv()

    sent = []

    def exchange(key, source, slots, peers, where):
        for j in peers:
            src, dst = source(j), slots(j)
            send(src, dst, r[key + "_send"], r[key + "_recv"], where(j))

    bufs = (r["p_sin"], r["p_out"], r["p_tin"], r["p_tout"])
    s_in, out, t_in, t_out = range(4)
    g_send, g_recv = r["g_send"], r["g_recv"]
    loaded("ts")
    line = lax.broadcasted_iota(jnp.int32, (SUB, rows_time), 0)
    lane = lax.broadcasted_iota(jnp.int32, (SUB, rows_time), 1)
    steps = jnp.zeros((SUB, rows_time), f32)
    for k in range(n_sam):
        value = r["ts"][k]
        steps = jnp.where(line == k, value.astype(f32), steps)
        steps = jnp.where(line == n_sam + k, (value - SKIP).astype(f32), steps)
    half_width = 4 * rows_time
    for d in range(8):
        place = (lane + (d % 4) * rows_time).astype(f32)
        angle = steps * jnp.exp(-math.log(10000.0) * place / half_width)
        wave = jax.nn.silu(jnp.cos(angle) if d < 4 else jnp.sin(angle))
        tf_own[d] = jnp.where(line < 2 * n_sam, wave.astype(bf16).astype(f32), 0.0)
    tf_all[pl.ds(me, 1)] = tf_own[pl.ds(me, 1)]
    loaded("sw")
    put_packed(bufs[s_in].at[me], sw[...])
    loaded("so", "to")
    for i in range(lo // 128):
        at, lanes = slice(i * rows_out, (i + 1) * rows_out), slice(i * 128, (i + 1) * 128)
        bufs[out][me, at, :] = so[:, lanes].astype(bf16)
        bufs[t_out][me, at, :] = to[:, lanes].astype(bf16)
    at = slice(lo // 128 * rows_out, (lo // 128 + 1) * rows_out)
    bufs[out][me, at, :] = jnp.concatenate([so[:, lo:], to[:, lo:]], axis=1).astype(bf16)
    loaded("tw")
    put_packed(bufs[t_in].at[me], tw[...])
    loaded("st", "tt")
    pl.semaphore_wait(barrier, 7 + n_rep - 1)

    def cut(seg):
        return bufs[seg].shape[1] // 32 * 16

    def push(seg, orel, t, r_at, start=0, count=None):
        count = bufs[seg].shape[1] if count is None else count
        part = bufs[seg].at[peer(orel), pl.ds(start, count)]
        send(part, part, g_send.at[seg], g_recv.at[seg * 4 + r_at], dp_id(t))

    def landed(seg, r_at, count=1):
        arrive(bufs[seg].at[pl.ds(0, count)], g_recv.at[seg * 4 + r_at])

    def open_gather(seg):
        push(seg, 0, 2, 0)
        push(seg, 0, 4, 1)
        push(seg, 0, 1, 3)
        sent.append((bufs[seg].at[pl.ds(0, 7)], g_send.at[seg]))

    def relay(seg):
        c = cut(seg)
        landed(seg, 0)
        push(seg, 2, 4, 2, 0, c)
        landed(seg, 1)
        push(seg, 4, 2, 2, c, bufs[seg].shape[1] - c)
        push(seg, 2, 1, 3)
        push(seg, 4, 1, 3)

    def relay_far(seg):
        landed(seg, 2)
        push(seg, 6, 1, 3)

    def close_gather(seg):
        landed(seg, 3, 4)

    def place_in(seg, dst):
        half = rows_in // 2
        for o in range(8):
            for i in range(lo // 128):
                dst[o * rows_in : (o + 1) * rows_in, i * 128 : (i + 1) * 128] = bufs[seg][
                    o, i * rows_in : (i + 1) * rows_in, :
                ]
            at = lo // 128 * rows_in
            tail = bufs[seg][o, at : at + half, :]
            dst[o * rows_in : o * rows_in + half, lo:] = tail[:, :rest]
            dst[o * rows_in + half : (o + 1) * rows_in, lo:] = tail[:, rest:]

    def place_out(seg, dst, first):
        for o in range(8):
            to_rows = slice(o * rows_out, (o + 1) * rows_out)
            for i in range(lo // 128):
                dst[to_rows, i * 128 : (i + 1) * 128] = bufs[seg][o, i * rows_out : (i + 1) * rows_out, :]
            at = lo // 128 * rows_out
            dst[to_rows, lo:] = bufs[out][o, at : at + rows_out, :][:, first : first + rest]

    near = (1, 2, 4, 3, 5, 6, 7)
    exchange("tf", lambda t: tf_own.at[peer(t)], lambda t: tf_all.at[me], near, dp_id)
    open_gather(s_in)
    st_b, tt_b = st[...].astype(bf16), tt[...].astype(bf16)
    arrive(tf_all.at[pl.ds(0, 7)], r["tf_recv"])
    feats = tf_all[...].reshape(8 * SUB, rows_time).astype(bf16)
    part_s = jnp.dot(feats, st_b, preferred_element_type=f32)
    part_t = jnp.dot(feats, tt_b, preferred_element_type=f32)
    which = lax.rem(lax.broadcasted_iota(jnp.int32, part_s.shape, 0), SUB)
    e_part[...] = jnp.where(which < n_sam, part_s, part_t).reshape(e_part.shape)
    e_in[pl.ds(me, 1)] = e_part[pl.ds(me, 1)]
    exchange("e", lambda t: e_part.at[peer(t)], lambda t: e_in.at[me], near, dp_id)
    relay(s_in)
    open_gather(out)
    open_gather(t_in)

    ft_all, em_all = r["ft_all"], r["em_all"]
    ft_all[pl.ds(rep, 1)] = jnp.concatenate([tf_all[d, :n_sam, :] for d in range(8)], axis=0).astype(bf16)[None]
    far = (3, 2, 1)
    exchange("ft", lambda j: ft_all.at[rep], lambda j: ft_all.at[rep], far, rep_id)
    start = 0
    for student, target in ((sw, tw), (so, to), (st, tt)):
        count = student.shape[0]
        e_all[start : start + count, :] = ema_decay * target[...] + (1.0 - ema_decay) * student[...]
        start += count
    loaded("x_s", "sg", "sb")

    arrive(e_in.at[pl.ds(0, 7)], r["e_recv"])
    emb = e_in[0]
    for k in range(1, 8):
        emb = emb + e_in[k]

    y_v, normed_v, inv_v, nb_v, nbt_v = (r[k] for k in ("y_v", "normed_v", "inv_v", "nb_v", "nbt_v"))
    hid_v, a_v, b_v, gyb_v, gm_v = (r[k] for k in ("hid_v", "a_v", "b_v", "gyb_v", "gm_v"))

    def normalise(x_ref, k, shift, gain, bias):
        summed = x_ref[:, pl.ds(k * per, per)].astype(f32).T + shift
        center = summed - jnp.mean(summed, axis=1, keepdims=True)
        inv = lax.rsqrt(jnp.mean(center * center, axis=1, keepdims=True) + 1e-05)
        normed = center * inv
        return summed, inv, normed, (normed * gain + bias).astype(bf16)

    for k in range(n_sam):
        at = pl.ds(k * per, per)
        summed, inv, normed, nb = normalise(x_s, k, emb[k : k + 1], sg[...][None], sb[...][None])
        y_v[at, :], normed_v[at, :], nb_v[at, :] = summed, normed, nb
        inv_v[at, :] = inv
    relay(out)
    open_gather(t_out)
    relay_far(s_in)
    loaded("x_t", "tg", "tb")
    for k in range(n_sam):
        at = pl.ds(k * per, per)
        summed, inv, normed, nb = normalise(
            x_t, k, emb[n_sam + k : n_sam + k + 1], tg[...][None], tb[...][None]
        )
        y_v[at, :], nbt_v[at, :] = y_v[at, :] - summed, nb
    close_gather(s_in)
    place_in(s_in, ws_all)

    for k in range(n_sam):
        at = pl.ds(k * per, per)
        gate = contract_last(nb_v[at, :], ws_all[:ff, :])
        up = contract_last(nb_v[at, :], ws_all[ff:, :])
        tangent = jnp.tanh(GATE_C * (gate + 0.044715 * gate * gate * gate))
        half = 0.5 * (1.0 + tangent)
        act = gate * half
        slope = half + 0.5 * gate * (1.0 - tangent * tangent) * GATE_C * (1.0 + 0.134145 * gate * gate)
        a_v[at, :], b_v[at, :] = up * slope, act
        hid_v[at, :] = (act * up).astype(bf16)
        if k == 0:
            relay(t_in)
            relay_far(out)
    relay(t_out)
    close_gather(out)
    place_out(out, os_all, 0)
    for k in range(n_sam):
        at = pl.ds(k * per, per)
        y_v[at, :] = y_v[at, :] + jnp.dot(hid_v[at, :], os_all[...], preferred_element_type=f32)
    relay_far(t_in)
    relay_far(t_out)
    close_gather(t_in)
    place_in(t_in, wt_all)

    for k in range(n_sam):
        at = pl.ds(k * per, per)
        gate = contract_last(nbt_v[at, :], wt_all[:ff, :])
        up = contract_last(nbt_v[at, :], wt_all[ff:, :])
        hid = (gelu_tanh(gate) * up).astype(bf16)
        if k == 0:
            close_gather(t_out)
            place_out(t_out, ot_all, rest)
        gy = (y_v[at, :] - jnp.dot(hid, ot_all[...], preferred_element_type=f32)) * (1.0 / tokens)
        y_v[at, :], gyb_v[at, :] = gy, gy.astype(bf16)

    r1_o, r1_i = r["r1_o"], r["r1_i"]
    blocks = {
        "o": (r["gs_o"], r1_o, rows_out, 0),
        "a": (r["gs_i"], r1_i, rows_in, 0),
        "b": (r["gs_i"], r1_i, rows_in, rows_out),
    }

    def to_core(src, dst, count, q, key):
        part = src.at[pl.ds(pl.multiple_of((2 * q + 1 - core) * count, 16), count)]
        send(part, dst.at[q], r[key + "_send"], r[key + "_recv"], dp_id(1))

    def pair(key, rel):
        g, r1, count, first = blocks[key]
        owner = peer(rel)
        own = g[pl.ds(pl.multiple_of(owner * count + first, 16), rows_out), :]
        return own + r1[lax.div(owner, 2), first : first + rows_out, :].astype(f32)

    def to_chip(key, k):
        s2, r2 = r["s2_" + key], r["r2_" + key]
        put_packed(s2.at[k], pair(key, 2 * k))
        send(s2.at[k], r2.at[k], r["r2s_" + key], r["r2r_" + key], dp_id(2 * k))

    total_out = contract_first(hid_v[...], gyb_v[...])
    r["gs_o"][...] = total_out
    r["gb_o"][...] = total_out.astype(bf16)
    for q in range(4):
        to_core(r["gb_o"], r1_o, rows_out, q, "c0")

    grad_gain = jnp.zeros((1, width), f32)
    grad_bias = grad_gain
    embs = []
    small, small_rep = r["small"], r["small_rep"]
    for k in range(n_sam):
        at = pl.ds(k * per, per)
        gh = contract_last(gyb_v[at, :], os_all[...])
        gma, gmb = (gh * a_v[at, :]).astype(bf16), (gh * b_v[at, :]).astype(bf16)
        gm_v[0, at, :], gm_v[1, at, :] = gma, gmb
        gz = jnp.dot(gma, ws_all[:ff, :], preferred_element_type=f32) + jnp.dot(
            gmb, ws_all[ff:, :], preferred_element_type=f32
        )
        normed = normed_v[at, :]
        grad_gain = grad_gain + jnp.sum(gz * normed, axis=0, keepdims=True)
        grad_bias = grad_bias + jnp.sum(gz, axis=0, keepdims=True)
        gn = gz * sg[...][None]
        gs = y_v[at, :] + inv_v[at, :] * (
            gn
            - jnp.mean(gn, axis=1, keepdims=True)
            - normed * jnp.mean(gn * normed, axis=1, keepdims=True)
        )
        embs.append(jnp.sum(gs, axis=0, keepdims=True))
        if k == 0:
            arrive(r1_o, r["c0_recv"])
            for q in (3, 1, 2):
                to_chip("o", q)
            put_packed(r["p_o"], pair("o", 0))
    fill = jnp.zeros((SUB - n_sam - 2, width), f32)
    small[pl.ds(me, 1)] = jnp.concatenate(embs + [grad_gain, grad_bias, fill], axis=0)[None]

    for turn in range(2):
        h = 1 - row if turn == 0 else row
        total = contract_first(gm_v[h], nb_v[...])
        at = pl.ds(pl.multiple_of(h * ff, 16), ff)
        r["gs_i"][at, :], r["gb_i"][at, :] = total, total.astype(bf16)
        for q in range(2):
            to_core(r["gb_i"], r1_i, rows_in, 2 * h + q, "c" + str(1 + turn))
        if turn == 0:
            exchange("sm", lambda t: small.at[me], lambda t: small.at[me], near, dp_id)
    arrive(r1_i.at[pl.ds(0, 2)], r["c1_recv"])
    for key in "ab":
        to_chip(key, 3)
        to_chip(key, 2)
    arrive(r1_i.at[pl.ds(0, 2)], r["c2_recv"])
    for key in "ab":
        to_chip(key, 1)
    for key in "ab":
        put_packed(r["p_" + key], pair(key, 0))

    def to_planes(key):
        p, pb, r2, r3 = r["p_" + key], r["pb_" + key], r["r2_" + key], r["r3_" + key]
        used, share = r2.shape[1], pb.shape[1]
        arrive(r2.at[pl.ds(1, 3)], r["r2r_" + key])
        p[:used, :] = p[:used, :] + r2[1].astype(f32) + r2[2].astype(f32) + r2[3].astype(f32)
        p[used:, :] = jnp.zeros((p.shape[0] - used, 128), f32)
        for q in range(n_rep):
            pb[q] = p[q * share : (q + 1) * share, :].astype(bf16)
        for j in far:
            send(pb.at[rep_peer(j)], r3.at[j], r["r3s_" + key], r["r3r_" + key], rep_id(j))

    def share_total(key):
        p, r3, fin = r["p_" + key], r["r3_" + key], r["fin_" + key]
        share = fin.shape[1]
        total = p[pl.ds(pl.multiple_of(rep * share, 8), share), :]
        arrive(r3.at[pl.ds(1, 3)], r["r3r_" + key])
        for j in range(1, n_rep):
            total = total + r3[j].astype(f32)
        fin[pl.ds(rep, 1)] = total.astype(bf16)[None]
        for j in far:
            send(fin.at[rep], fin.at[rep], r["r4s_" + key], r["r4r_" + key], rep_id(j))

    def finish(start, grad):
        at = slice(start, start + grad.shape[0])
        g_all[at, :] = grad
        e_all[at, :] = e_all[at, :] - (1.0 - ema_decay) * learn_rate * grad

    def collect(key, start):
        p, fin = r["p_" + key], r["fin_" + key]
        share = fin.shape[1]
        arrive(fin.at[pl.ds(0, 3)], r["r4r_" + key])
        for q in range(n_rep):
            p[q * share : (q + 1) * share, :] = fin[q].astype(f32)
        finish(start, unpacked(p[...], rows_out, width))

    to_planes("o")
    arrive(small.at[pl.ds(0, 7)], r["sm_recv"])
    em_all[pl.ds(rep, 1)] = jnp.concatenate([small[d, :n_sam, :] for d in range(8)], axis=0).astype(bf16)[None]
    sums = small[0]
    for k in range(1, 8):
        sums = sums + small[k]
    small_rep[pl.ds(rep, 1)] = sums[None]
    exchange("em", lambda j: em_all.at[rep], lambda j: em_all.at[rep], far, rep_id)
    exchange("rs", lambda j: small_rep.at[rep], lambda j: small_rep.at[rep], far, rep_id)
    share_total("o")
    to_planes("a")
    arrive(ft_all.at[pl.ds(0, 3)], r["ft_recv"])
    arrive(em_all.at[pl.ds(0, 3)], r["em_recv"])
    arrive(small_rep.at[pl.ds(0, 3)], r["rs_recv"])
    grad_time = contract_first(ft_all[0], em_all[0])
    sums = small_rep[0]
    for j in range(1, n_rep):
        grad_time = grad_time + contract_first(ft_all[j], em_all[j])
        sums = sums + small_rep[j]
    finish(rows_in + rows_out, grad_time)
    gg, gb = sums[n_sam, :], sums[n_sam + 1, :]
    r["gg_o"][...], r["gb_o_"][...] = gg, gb
    r["eg_o"][...] = average(tg[...], sg[...], gg)
    r["eb_o"][...] = average(tb[...], sb[...], gb)
    to_planes("b")
    collect("o", rows_in)
    share_total("a")
    share_total("b")
    collect("a", 0)
    collect("b", rows_out)
    for key, ref in (("tf", tf_all), ("e", e_in), ("sm", small)):
        sent.append((ref.at[pl.ds(0, 7)], r[key + "_send"]))
    for key, ref in (("ft", ft_all), ("em", em_all), ("rs", small_rep)):
        sent.append((ref.at[pl.ds(0, 3)], r[key + "_send"]))
    sent += [(r1_o, r["c0_send"]), (r1_i.at[pl.ds(0, 2)], r["c1_send"]), (r1_i.at[pl.ds(0, 2)], r["c2_send"])]
    for key in "oab":
        sent.append((r["r2_" + key].at[pl.ds(0, 3)], r["r2s_" + key]))
        sent.append((r["r3_" + key].at[pl.ds(0, 3)], r["r3s_" + key]))
        sent.append((r["fin_" + key].at[pl.ds(0, 3)], r["r4s_" + key]))
    for ref, sem in sent:
        bytes_of(ref, sem).wait_send()


LOADED = ("ts", "sw", "so", "to", "tw", "st", "tt", "x_s", "sg", "sb", "x_t", "tg", "tb")


def average(target_p, student_p, grad_p):
    return ema_decay * target_p + (1.0 - ema_decay) * (student_p - learn_rate * grad_p)


def output_kernel(grads, means, gg, gb, eg, eb, gw_o, go_o, gt_o, gg_o, gb_o, ew_o, eo_o, et_o, eg_o, eb_o, sem):
    copies = []
    for src, outs in ((grads, (gw_o, go_o, gt_o)), (means, (ew_o, eo_o, et_o))):
        start = 0
        for dst in outs:
            copies.append((src.at[pl.ds(start, dst.shape[0])], dst))
            start += dst.shape[0]
    copies += [(gg, gg_o), (gb, gb_o), (eg, eg_o), (eb, eb_o)]
    copies = [pltpu.make_async_copy(src, dst, sem.at[i]) for i, (src, dst) in enumerate(copies)]
    for copy in copies:
        copy.start()
    for copy in copies:
        copy.wait()


def fused_device(n_dp, n_rep, *args):
    (student_in, target_in, timesteps, sw, so, st, sg, sb, tw, to, tt, tg, tb) = args
    f32, bf16 = jnp.float32, jnp.bfloat16
    tokens, width = student_in.shape
    n_sam = timesteps.shape[0]
    rows_in, rows_out, rows_time = sw.shape[0], so.shape[0], st.shape[0]
    ff = rows_out * n_dp
    rows_all = rows_in + rows_out + rows_time
    vm = pltpu.VMEM
    dma = pltpu.SemaphoreType.DMA
    full = width // 128
    packed_in, packed_out = rows_in * full + rows_in // 2, rows_out * full + rows_out // 2
    share = -(-packed_out // (8 * n_rep)) * 8
    scratch = dict(
        ts=pltpu.SMEM((n_sam,), jnp.int32),
        sw=vm(sw.shape, f32), so=vm(so.shape, f32), st=vm(st.shape, f32),
        tw=vm(tw.shape, f32), to=vm(to.shape, f32), tt=vm(tt.shape, f32),
        sg=vm(sg.shape, f32), sb=vm(sb.shape, f32), tg=vm(tg.shape, f32), tb=vm(tb.shape, f32),
        x_s=vm((width, tokens), bf16), x_t=vm((width, tokens), bf16),
        p_sin=vm((n_dp, packed_in, 128), bf16), p_out=vm((n_dp, rows_out * (full + 1), 128), bf16),
        p_tin=vm((n_dp, packed_in, 128), bf16), p_tout=vm((n_dp, rows_out * full, 128), bf16),
        ws_all=vm((n_dp * rows_in, width), bf16), os_all=vm((ff, width), bf16),
        wt_all=vm((n_dp * rows_in, width), bf16), ot_all=vm((ff, width), bf16),
        tf_own=vm((n_dp, SUB, rows_time), f32), tf_all=vm((n_dp, SUB, rows_time), f32),
        e_part=vm((n_dp, SUB, width), f32), e_in=vm((n_dp, SUB, width), f32),
        small=vm((n_dp, SUB, width), f32), small_rep=vm((n_rep, SUB, width), f32),
        ft_all=vm((n_rep, n_dp * n_sam, rows_time), bf16), em_all=vm((n_rep, n_dp * n_sam, width), bf16),
        normed_v=vm((tokens, width), f32), inv_v=vm((tokens, 1), f32), nb_v=vm((tokens, width), bf16),
        hid_v=vm((tokens, ff), bf16), a_v=vm((tokens, ff), f32), b_v=vm((tokens, ff), f32),
        y_v=vm((tokens, width), f32), nbt_v=vm((tokens, width), bf16), gyb_v=vm((tokens, width), bf16),
        gm_v=vm((2, tokens, ff), bf16),
        gs_i=vm((n_dp * rows_in, width), f32), gs_o=vm((ff, width), f32),
        gb_i=vm((n_dp * rows_in, width), bf16), gb_o=vm((ff, width), bf16),
        r1_i=vm((4, rows_in, width), bf16), r1_o=vm((4, rows_out, width), bf16),
        ld_sem=dma((len(LOADED),)), g_send=dma((4,)), g_recv=dma((16,)),
    )
    for key in "oab":
        for name in ("s2_", "r2_"):
            scratch[name + key] = vm((4, packed_out, 128), bf16)
        scratch["p_" + key] = vm((n_rep * share, 128), f32)
        for name in ("pb_", "r3_", "fin_"):
            scratch[name + key] = vm((n_rep, share, 128), bf16)
        for name in ("r2", "r3", "r4"):
            scratch[name + "s_" + key], scratch[name + "r_" + key] = dma, dma
    for key in ("tf", "e", "sm", "ft", "em", "rs", "c0", "c1", "c2"):
        scratch[key + "_send"], scratch[key + "_recv"] = dma, dma
    shape = jax.ShapeDtypeStruct
    results = dict(
        g_o=shape((rows_all, width), f32), e_o=shape((rows_all, width), f32), gg_o=shape((width,), f32),
        gb_o_=shape((width,), f32), eg_o=shape((width,), f32), eb_o=shape((width,), f32),
    )
    operands = dict(
        ts=timesteps, sw=sw, so=so, to=to, tw=tw, st=st, tt=tt, x_s=student_in.T, sg=sg, sb=sb,
        x_t=target_in.T, tg=tg, tb=tb,
    )
    names = tuple(key + "_h" for key in operands) + tuple(results) + tuple(scratch)
    values = pl.pallas_call(
        functools.partial(fused_kernel, n_rep, n_sam, names),
        out_shape=tuple(results.values()),
        in_specs=[pl.BlockSpec(memory_space=pltpu.HBM)] * len(operands),
        out_specs=[pl.BlockSpec(memory_space=vm)] * len(results),
        scratch_shapes=list(scratch.values()),
        compiler_params=pltpu.CompilerParams(
            collective_id=0, has_side_effects=True, vmem_limit_bytes=40 * 1024 * 1024
        ),
        name="distill_step",
    )(*(pltpu.with_memory_space_constraint(value, pltpu.HBM) for value in operands.values()))
    big = [shape(w.shape, f32) for w in (sw, so, st)]
    flat = [shape((width,), f32)] * 2
    return tuple(
        pl.pallas_call(
            output_kernel,
            out_shape=(*big, *flat, *big, *flat),
            in_specs=[pl.BlockSpec(memory_space=vm)] * len(results),
            out_specs=[pl.BlockSpec(memory_space=pltpu.HBM)] * 10,
            scratch_shapes=[dma((10,))],
            compiler_params=pltpu.CompilerParams(vmem_limit_bytes=8 * 1024 * 1024),
            name="output_step",
        )(*values)
    )


def fits_fused(n_dp, n_rep, args):
    tokens, samples = args[0].shape[0], args[2].shape[0]
    n_dev = n_dp * n_rep
    rows = [args[i].shape[0] for i in (3, 4, 5)]
    return (
        n_dp == 8
        and n_rep == 4
        and samples % n_dev == 0
        and 2 * (samples // n_dev) + 0 <= SUB
        and samples // n_dev + 2 <= SUB
        and tokens % samples == 0
        and (tokens // samples) % 128 == 0
        and all(r % (16 * n_dp) == 0 for r in rows)
        and all(r % (32 * n_dp) == 0 for r in rows[:1])
        and rows[0] == 2 * rows[1]
        and rows[2] == rows[1]
        and args[0].shape[1] % 128 == 64
    )


def solution(mesh):
    in_specs = (
        P(("dp", "rep"), None),
        P(("dp", "rep"), None),
        P(("dp", "rep")),
        P("dp", None),
        P("dp", None),
        P("dp", None),
        P(),
        P(),
        P("dp", None),
        P("dp", None),
        P("dp", None),
        P(),
        P(),
    )
    out_specs = (
        P("dp", None),
        P("dp", None),
        P("dp", None),
        P(),
        P(),
        P("dp", None),
        P("dp", None),
        P("dp", None),
        P(),
        P(),
    )
    n_dp, n_rep = mesh.shape["dp"], mesh.shape["rep"]

    def step(*args):
        fused = fits_fused(n_dp, n_rep, args)
        body = functools.partial(fused_device, n_dp, n_rep) if fused else per_device
        return jax.shard_map(
            body, mesh=mesh, in_specs=in_specs, out_specs=out_specs, check_vma=False
        )(*args)

    return step
```

time: 67.1 us -> 46.5 us (0.69)
  Pallas kernels: 64.5 us -> 45.7 us
  local copies, waits for them, and re-layouts: 1.35 us -> 0 us
    pallas_call x2, Pallas kernels: 64.5 us -> 45.7 us  [the longest x1 44.6 us: fused_device(): pl.pallas_call(functools.partial(fused_kernel, n_rep, n_sam, names), out_...]
    transpose x2 -> x0, local copies, waits for them, and re-layouts: 0.7 us -> none  [fused_device(): feats = feats.reshape(SUB, n_dp, rows_time).transpose(1, 0, 2)]
where the time goes in v1:
time: 46.5 us; the launch traced here: 46.3 us
  Pallas kernels  45.7 us (98%)
  between operations  0.66 us (1%)
    pallas_call x1, Pallas kernels, fused_device(): pl.pallas_call(functools.partial(fused_kernel, n_rep, n_sam, names), out_...  44.6 us
    pallas_call x1, Pallas kernels, fused_device(): pl.pallas_call(output_kernel, out_shape=(*big, *flat, *big, *flat), in_sp...  1.03 us

profile of v1, /device:TPU:0, one launch (start us, length us, event | category | flops | bytes accessed | tf_op | source)
XLA Modules:
  0.0 46.3 jit_solution(6568369066535832025)
XLA Ops:
  0.6 44.6 %distill_step.1 = (f32[320,320]{1,0:T(8,128)S(1)}, f32[320,320]{1,0:T(8,128)S(1)}, f32[320]{0:T(512)S(1)}, f32[320]{0:T(512)S(1)}, f32[320]{0:T(512)S(1)}, /*index=5*/f32[320]{0:T(512)S(1)}) custom-call(s32[2]{0:T(128)} %refs_0_.1, f32[160,320]{1,0:T(8,128)} %refs_1_.1, f32[80,320]{1,0:T(8,128)} %refs_2_.1, f32[80,320]{1,0:T(8,128)} %refs_3_.1, ...), custom_call_target="tpu_custom_call" | custom-call | tf_op jit(solution)/shard_map/distill_step/pallas_call | solution.py:682
  45.3 1.0 %output_step.1 = (f32[160,320]{1,0:T(8,128)}, f32[80,320]{1,0:T(8,128)}, f32[80,320]{1,0:T(8,128)}, f32[320]{0:T(512)}, f32[320]{0:T(512)}, /*index=5*/f32[160,3...) custom-call(f32[320,320]{1,0:T(8,128)S(1)} %get-tuple-element.16.grads, ...), custom_call_target="tpu_custom_call" | custom-call | tf_op jit(solution)/shard_map/output_step/pallas_call | solution.py:696

commit v2 on v1

--- a/solution.py
+++ b/solution.py
@@ -205,6 +205,7 @@
     sw, so, st, tw, to, tt = (r[k] for k in ("sw", "so", "st", "tw", "to", "tt"))
     sg, sb, tg, tb, x_s, x_t = (r[k] for k in ("sg", "sb", "tg", "tb", "x_s", "x_t"))
     rows_in, rows_out, rows_time = sw.shape[0], so.shape[0], st.shape[0]
+    packed_out = r["s2_a"].shape[1]
     width, tokens = x_s.shape
     per = tokens // n_sam
     lo = width // 128 * 128
@@ -354,6 +355,7 @@
     near = (1, 2, 4, 3, 5, 6, 7)
     exchange("tf", lambda t: tf_own.at[peer(t)], lambda t: tf_all.at[me], near, dp_id)
     open_gather(s_in)
+    open_gather(t_in)
     st_b, tt_b = st[...].astype(bf16), tt[...].astype(bf16)
     arrive(tf_all.at[pl.ds(0, 7)], r["tf_recv"])
     feats = tf_all[...].reshape(8 * SUB, rows_time).astype(bf16)
@@ -365,7 +367,6 @@
     exchange("e", lambda t: e_part.at[peer(t)], lambda t: e_in.at[me], near, dp_id)
     relay(s_in)
     open_gather(out)
-    open_gather(t_in)
 
     ft_all, em_all = r["ft_all"], r["em_all"]
     ft_all[pl.ds(rep, 1)] = jnp.concatenate([tf_all[d, :n_sam, :] for d in range(8)], axis=0).astype(bf16)[None]
@@ -376,7 +377,10 @@
         count = student.shape[0]
         e_all[start : start + count, :] = ema_decay * target[...] + (1.0 - ema_decay) * student[...]
         start += count
+    relay(t_in)
+    open_gather(t_out)
     loaded("x_s", "sg", "sb")
+    relay_far(s_in)
 
     arrive(e_in.at[pl.ds(0, 7)], r["e_recv"])
     emb = e_in[0]
@@ -384,7 +388,7 @@
         emb = emb + e_in[k]
 
     y_v, normed_v, inv_v, nb_v, nbt_v = (r[k] for k in ("y_v", "normed_v", "inv_v", "nb_v", "nbt_v"))
-    hid_v, a_v, b_v, gyb_v, gm_v = (r[k] for k in ("hid_v", "a_v", "b_v", "gyb_v", "gm_v"))
+    hid_v, hidt_v, a_v, b_v, gyb_v, gm_v = (r[k] for k in ("hid_v", "hidt_v", "a_v", "b_v", "gyb_v", "gm_v"))
 
     def normalise(x_ref, k, shift, gain, bias):
         summed = x_ref[:, pl.ds(k * per, per)].astype(f32).T + shift
@@ -398,9 +402,6 @@
         summed, inv, normed, nb = normalise(x_s, k, emb[k : k + 1], sg[...][None], sb[...][None])
         y_v[at, :], normed_v[at, :], nb_v[at, :] = summed, normed, nb
         inv_v[at, :] = inv
-    relay(out)
-    open_gather(t_out)
-    relay_far(s_in)
     loaded("x_t", "tg", "tb")
     for k in range(n_sam):
         at = pl.ds(k * per, per)
@@ -408,6 +409,7 @@
             x_t, k, emb[n_sam + k : n_sam + k + 1], tg[...][None], tb[...][None]
         )
         y_v[at, :], nbt_v[at, :] = y_v[at, :] - summed, nb
+    relay(out)
     close_gather(s_in)
     place_in(s_in, ws_all)
 
@@ -422,28 +424,27 @@
         a_v[at, :], b_v[at, :] = up * slope, act
         hid_v[at, :] = (act * up).astype(bf16)
         if k == 0:
-            relay(t_in)
-            relay_far(out)
+            relay_far(t_in)
     relay(t_out)
-    close_gather(out)
-    place_out(out, os_all, 0)
-    for k in range(n_sam):
-        at = pl.ds(k * per, per)
-        y_v[at, :] = y_v[at, :] + jnp.dot(hid_v[at, :], os_all[...], preferred_element_type=f32)
-    relay_far(t_in)
-    relay_far(t_out)
+    relay_far(out)
     close_gather(t_in)
     place_in(t_in, wt_all)
-
     for k in range(n_sam):
         at = pl.ds(k * per, per)
         gate = contract_last(nbt_v[at, :], wt_all[:ff, :])
         up = contract_last(nbt_v[at, :], wt_all[ff:, :])
-        hid = (gelu_tanh(gate) * up).astype(bf16)
-        if k == 0:
-            close_gather(t_out)
-            place_out(t_out, ot_all, rest)
-        gy = (y_v[at, :] - jnp.dot(hid, ot_all[...], preferred_element_type=f32)) * (1.0 / tokens)
+        hidt_v[at, :] = (gelu_tanh(gate) * up).astype(bf16)
+    close_gather(out)
+    place_out(out, os_all, 0)
+    relay_far(t_out)
+    for k in range(n_sam):
+        at = pl.ds(k * per, per)
+        y_v[at, :] = y_v[at, :] + jnp.dot(hid_v[at, :], os_all[...], preferred_element_type=f32)
+    close_gather(t_out)
+    place_out(t_out, ot_all, rest)
+    for k in range(n_sam):
+        at = pl.ds(k * per, per)
+        gy = (y_v[at, :] - jnp.dot(hidt_v[at, :], ot_all[...], preferred_element_type=f32)) * (1.0 / tokens)
         y_v[at, :], gyb_v[at, :] = gy, gy.astype(bf16)
 
     r1_o, r1_i = r["r1_o"], r["r1_i"]
@@ -474,21 +475,30 @@
     for q in range(4):
         to_core(r["gb_o"], r1_o, rows_out, q, "c0")
 
+    for k in range(n_sam):
+        at = pl.ds(k * per, per)
+        gh = contract_last(gyb_v[at, :], os_all[...])
+        gm_v[0, at, :], gm_v[1, at, :] = (gh * a_v[at, :]).astype(bf16), (gh * b_v[at, :]).astype(bf16)
+
+    def weight_grad(turn):
+        h = 1 - row if turn == 0 else row
+        total = contract_first(gm_v[h], nb_v[...])
+        at = pl.ds(pl.multiple_of(h * ff, 16), ff)
+        r["gs_i"][at, :], r["gb_i"][at, :] = total, total.astype(bf16)
+        for q in range(2):
+            to_core(r["gb_i"], r1_i, rows_in, 2 * h + q, "c" + str(1 + turn))
+
     grad_gain = jnp.zeros((1, width), f32)
     grad_bias = grad_gain
     embs = []
     small, small_rep = r["small"], r["small_rep"]
-    for k in range(n_sam):
+
+    def input_grad(k):
         at = pl.ds(k * per, per)
-        gh = contract_last(gyb_v[at, :], os_all[...])
-        gma, gmb = (gh * a_v[at, :]).astype(bf16), (gh * b_v[at, :]).astype(bf16)
-        gm_v[0, at, :], gm_v[1, at, :] = gma, gmb
-        gz = jnp.dot(gma, ws_all[:ff, :], preferred_element_type=f32) + jnp.dot(
-            gmb, ws_all[ff:, :], preferred_element_type=f32
+        gz = jnp.dot(gm_v[0, at, :], ws_all[:ff, :], preferred_element_type=f32) + jnp.dot(
+            gm_v[1, at, :], ws_all[ff:, :], preferred_element_type=f32
         )
         normed = normed_v[at, :]
-        grad_gain = grad_gain + jnp.sum(gz * normed, axis=0, keepdims=True)
-        grad_bias = grad_bias + jnp.sum(gz, axis=0, keepdims=True)
         gn = gz * sg[...][None]
         gs = y_v[at, :] + inv_v[at, :] * (
             gn
@@ -496,30 +506,38 @@
             - normed * jnp.mean(gn * normed, axis=1, keepdims=True)
         )
         embs.append(jnp.sum(gs, axis=0, keepdims=True))
+        return jnp.sum(gz * normed, axis=0, keepdims=True), jnp.sum(gz, axis=0, keepdims=True)
+
+    weight_grad(0)
+    arrive(r1_o, r["c0_recv"])
+    z_v, zb_v, rz_v = r["z_v"], r["zb_v"], r["rz_v"]
+    share = rz_v.shape[2]
+    for q in range(4):
+        own = r["gs_o"][pl.ds(pl.multiple_of((2 * q + core) * rows_out, 16), rows_out), :]
+        put_packed(z_v.at[q], own + r1_o[q].astype(f32))
+        z_v[q, packed_out:, :] = jnp.zeros((z_v.shape[1] - packed_out, 128), f32)
+        for j in range(n_rep):
+            zb_v[j, q] = z_v[q, j * share : (j + 1) * share, :].astype(bf16)
+    exchange("rz", lambda j: zb_v.at[rep_peer(j)], lambda j: rz_v.at[j], far, rep_id)
+    weight_grad(1)
+    for k in range(n_sam):
+        more_gain, more_bias = input_grad(k)
+        grad_gain, grad_bias = grad_gain + more_gain, grad_bias + more_bias
         if k == 0:
-            arrive(r1_o, r["c0_recv"])
-            for q in (3, 1, 2):
-                to_chip("o", q)
-            put_packed(r["p_o"], pair("o", 0))
-    fill = jnp.zeros((SUB - n_sam - 2, width), f32)
-    small[pl.ds(me, 1)] = jnp.concatenate(embs + [grad_gain, grad_bias, fill], axis=0)[None]
-
-    for turn in range(2):
-        h = 1 - row if turn == 0 else row
-        total = contract_first(gm_v[h], nb_v[...])
-        at = pl.ds(pl.multiple_of(h * ff, 16), ff)
-        r["gs_i"][at, :], r["gb_i"][at, :] = total, total.astype(bf16)
-        for q in range(2):
-            to_core(r["gb_i"], r1_i, rows_in, 2 * h + q, "c" + str(1 + turn))
-        if turn == 0:
-            exchange("sm", lambda t: small.at[me], lambda t: small.at[me], near, dp_id)
-    arrive(r1_i.at[pl.ds(0, 2)], r["c1_recv"])
-    for key in "ab":
-        to_chip(key, 3)
-        to_chip(key, 2)
+            arrive(r1_i.at[pl.ds(0, 2)], r["c1_recv"])
+            to_chip("a", 3)
+            to_chip("a", 2)
     arrive(r1_i.at[pl.ds(0, 2)], r["c2_recv"])
-    for key in "ab":
-        to_chip(key, 1)
+    to_chip("a", 1)
+    high = [v.astype(bf16).astype(f32) for v in (grad_gain, grad_bias)]
+    low = [v - h for v, h in zip((grad_gain, grad_bias), high)]
+    n_small = n_sam + 4
+    r["pack_v"][...] = jnp.zeros(r["pack_v"].shape, f32)
+    put_packed(r["pack_v"], jnp.concatenate(embs + high + low, axis=0))
+    small[pl.ds(me, 1)] = r["pack_v"][...].astype(bf16)[None]
+    exchange("sm", lambda t: small.at[me], lambda t: small.at[me], near, dp_id)
+    for k in (3, 2, 1):
+        to_chip("b", k)
     for key in "ab":
         put_packed(r["p_" + key], pair(key, 0))
 
@@ -534,6 +552,32 @@
         for j in far:
             send(pb.at[rep_peer(j)], r3.at[j], r["r3s_" + key], r["r3r_" + key], rep_id(j))
 
+    def plane_total():
+        arrive(rz_v.at[pl.ds(1, 3)], r["rz_recv"])
+        tz_v, tzb_v = r["tz_v"], r["tzb_v"]
+        for q in range(4):
+            total = z_v[q, pl.ds(pl.multiple_of(rep * share, 8), share), :]
+            for j in range(1, n_rep):
+                total = total + rz_v[j, q].astype(f32)
+            tz_v[q], tzb_v[q] = total, total.astype(bf16)
+        exchange(
+            "r2z", lambda k: tzb_v.at[lax.div(peer(2 * k), 2)], lambda k: r["r2z_v"].at[k], (3, 1, 2),
+            lambda k: dp_id(2 * k),
+        )
+
+    def chip_total():
+        arrive(r["r2z_v"].at[pl.ds(1, 3)], r["r2z_recv"])
+        total = r["tz_v"][lax.div(me, 2)]
+        for k in (1, 2, 3):
+            total = total + r["r2z_v"][k].astype(f32)
+        spread("o", total)
+
+    def spread(key, total):
+        fin = r["fin_" + key]
+        fin[pl.ds(rep, 1)] = total.astype(bf16)[None]
+        for j in far:
+            send(fin.at[rep], fin.at[rep], r["r4s_" + key], r["r4r_" + key], rep_id(j))
+
     def share_total(key):
         p, r3, fin = r["p_" + key], r["r3_" + key], r["fin_" + key]
         share = fin.shape[1]
@@ -541,9 +585,7 @@
         arrive(r3.at[pl.ds(1, 3)], r["r3r_" + key])
         for j in range(1, n_rep):
             total = total + r3[j].astype(f32)
-        fin[pl.ds(rep, 1)] = total.astype(bf16)[None]
-        for j in far:
-            send(fin.at[rep], fin.at[rep], r["r4s_" + key], r["r4r_" + key], rep_id(j))
+        spread(key, total)
 
     def finish(start, grad):
         at = slice(start, start + grad.shape[0])
@@ -558,34 +600,43 @@
             p[q * share : (q + 1) * share, :] = fin[q].astype(f32)
         finish(start, unpacked(p[...], rows_out, width))
 
-    to_planes("o")
+    to_planes("a")
     arrive(small.at[pl.ds(0, 7)], r["sm_recv"])
-    em_all[pl.ds(rep, 1)] = jnp.concatenate([small[d, :n_sam, :] for d in range(8)], axis=0).astype(bf16)[None]
-    sums = small[0]
+    part = [small[d].astype(f32) for d in range(8)]
+    em_all[pl.ds(rep, 1)] = jnp.concatenate(
+        [unpacked(p, n_small, width)[:n_sam] for p in part], axis=0
+    ).astype(bf16)[None]
+    sums = part[0]
     for k in range(1, 8):
-        sums = sums + small[k]
-    small_rep[pl.ds(rep, 1)] = sums[None]
+        sums = sums + part[k]
+    sums = unpacked(sums, n_small, width)
+    sums = sums[n_sam : n_sam + 2] + sums[n_sam + 2 : n_sam + 4]
+    high = sums.astype(bf16).astype(f32)
+    put_packed(r["pack_v"], jnp.concatenate([high, sums - high], axis=0))
+    small_rep[pl.ds(rep, 1)] = r["pack_v"][...].astype(bf16)[None]
     exchange("em", lambda j: em_all.at[rep], lambda j: em_all.at[rep], far, rep_id)
     exchange("rs", lambda j: small_rep.at[rep], lambda j: small_rep.at[rep], far, rep_id)
-    share_total("o")
-    to_planes("a")
+    plane_total()
+    to_planes("b")
+    share_total("a")
+    chip_total()
     arrive(ft_all.at[pl.ds(0, 3)], r["ft_recv"])
     arrive(em_all.at[pl.ds(0, 3)], r["em_recv"])
     arrive(small_rep.at[pl.ds(0, 3)], r["rs_recv"])
     grad_time = contract_first(ft_all[0], em_all[0])
-    sums = small_rep[0]
+    sums = jnp.zeros((2, width), f32)
+    for j in range(n_rep):
+        part = unpacked(small_rep[j].astype(f32), 4, width)
+        sums = sums + part[:2] + part[2:]
     for j in range(1, n_rep):
         grad_time = grad_time + contract_first(ft_all[j], em_all[j])
-        sums = sums + small_rep[j]
     finish(rows_in + rows_out, grad_time)
-    gg, gb = sums[n_sam, :], sums[n_sam + 1, :]
+    gg, gb = sums[0, :], sums[1, :]
     r["gg_o"][...], r["gb_o_"][...] = gg, gb
     r["eg_o"][...] = average(tg[...], sg[...], gg)
     r["eb_o"][...] = average(tb[...], sb[...], gb)
-    to_planes("b")
+    share_total("b")
     collect("o", rows_in)
-    share_total("a")
-    share_total("b")
     collect("a", 0)
     collect("b", rows_out)
     for key, ref in (("tf", tf_all), ("e", e_in), ("sm", small)):
@@ -593,9 +644,11 @@
     for key, ref in (("ft", ft_all), ("em", em_all), ("rs", small_rep)):
         sent.append((ref.at[pl.ds(0, 3)], r[key + "_send"]))
     sent += [(r1_o, r["c0_send"]), (r1_i.at[pl.ds(0, 2)], r["c1_send"]), (r1_i.at[pl.ds(0, 2)], r["c2_send"])]
-    for key in "oab":
+    for key in "ab":
         sent.append((r["r2_" + key].at[pl.ds(0, 3)], r["r2s_" + key]))
         sent.append((r["r3_" + key].at[pl.ds(0, 3)], r["r3s_" + key]))
+    sent += [(rz_v.at[pl.ds(0, 3)], r["rz_send"]), (r["r2z_v"].at[pl.ds(0, 3)], r["r2z_send"])]
+    for key in "oab":
         sent.append((r["fin_" + key].at[pl.ds(0, 3)], r["r4s_" + key]))
     for ref, sem in sent:
         bytes_of(ref, sem).wait_send()
@@ -634,6 +687,7 @@
     vm = pltpu.VMEM
     dma = pltpu.SemaphoreType.DMA
     full = width // 128
+    rows_small = -(-((n_sam + 4) * full + (n_sam + 4) // 2) // 16) * 16
     packed_in, packed_out = rows_in * full + rows_in // 2, rows_out * full + rows_out // 2
     share = -(-packed_out // (8 * n_rep)) * 8
     scratch = dict(
@@ -648,10 +702,10 @@
         wt_all=vm((n_dp * rows_in, width), bf16), ot_all=vm((ff, width), bf16),
         tf_own=vm((n_dp, SUB, rows_time), f32), tf_all=vm((n_dp, SUB, rows_time), f32),
         e_part=vm((n_dp, SUB, width), f32), e_in=vm((n_dp, SUB, width), f32),
-        small=vm((n_dp, SUB, width), f32), small_rep=vm((n_rep, SUB, width), f32),
+        small=vm((n_dp, rows_small, 128), bf16), pack_v=vm((rows_small, 128), f32), small_rep=vm((n_rep, rows_small, 128), bf16),
         ft_all=vm((n_rep, n_dp * n_sam, rows_time), bf16), em_all=vm((n_rep, n_dp * n_sam, width), bf16),
         normed_v=vm((tokens, width), f32), inv_v=vm((tokens, 1), f32), nb_v=vm((tokens, width), bf16),
-        hid_v=vm((tokens, ff), bf16), a_v=vm((tokens, ff), f32), b_v=vm((tokens, ff), f32),
+        hid_v=vm((tokens, ff), bf16), hidt_v=vm((tokens, ff), bf16), a_v=vm((tokens, ff), f32), b_v=vm((tokens, ff), f32),
         y_v=vm((tokens, width), f32), nbt_v=vm((tokens, width), bf16), gyb_v=vm((tokens, width), bf16),
         gm_v=vm((2, tokens, ff), bf16),
         gs_i=vm((n_dp * rows_in, width), f32), gs_o=vm((ff, width), f32),
@@ -660,14 +714,23 @@
         ld_sem=dma((len(LOADED),)), g_send=dma((4,)), g_recv=dma((16,)),
     )
     for key in "oab":
+        scratch["p_" + key] = vm((n_rep * share, 128), f32)
+        scratch["fin_" + key] = vm((n_rep, share, 128), bf16)
+        scratch["r4s_" + key], scratch["r4r_" + key] = dma, dma
+    for key in "ab":
         for name in ("s2_", "r2_"):
             scratch[name + key] = vm((4, packed_out, 128), bf16)
-        scratch["p_" + key] = vm((n_rep * share, 128), f32)
-        for name in ("pb_", "r3_", "fin_"):
+        for name in ("pb_", "r3_"):
             scratch[name + key] = vm((n_rep, share, 128), bf16)
-        for name in ("r2", "r3", "r4"):
+        for name in ("r2", "r3"):
             scratch[name + "s_" + key], scratch[name + "r_" + key] = dma, dma
-    for key in ("tf", "e", "sm", "ft", "em", "rs", "c0", "c1", "c2"):
+    scratch["z_v"] = vm((4, n_rep * share, 128), f32)
+    for name in ("zb_v", "rz_v"):
+        scratch[name] = vm((n_rep, 4, share, 128), bf16)
+    scratch["tz_v"] = vm((4, share, 128), f32)
+    for name in ("tzb_v", "r2z_v"):
+        scratch[name] = vm((4, share, 128), bf16)
+    for key in ("tf", "e", "sm", "ft", "em", "rs", "c0", "c1", "c2", "rz", "r2z"):
         scratch[key + "_send"], scratch[key + "_recv"] = dma, dma
     shape = jax.ShapeDtypeStruct
     results = dict(
@@ -714,7 +777,7 @@
         and n_rep == 4
         and samples % n_dev == 0
         and 2 * (samples // n_dev) + 0 <= SUB
-        and samples // n_dev + 2 <= SUB
+        and (samples // n_dev) % 2 == 0
         and tokens % samples == 0
         and (tokens // samples) % 128 == 0
         and all(r % (16 * n_dp) == 0 for r in rows)

time: 46.5 us -> 43.1 us (0.927)
  Pallas kernels: 45.7 us -> 42.3 us
    pallas_call x1, Pallas kernels: 44.6 us -> 41.3 us  [fused_device(): pl.pallas_call(functools.partial(fused_kernel, n_rep, n_sam, names), out_...]
where the time goes in v2:
time: 43.1 us; the launch traced here: 43 us
  Pallas kernels  42.3 us (98%)
  between operations  0.66 us (2%)
    pallas_call x1, Pallas kernels, fused_device(): pl.pallas_call(functools.partial(fused_kernel, n_rep, n_sam, names), out_...  41.3 us
    pallas_call x1, Pallas kernels, fused_device(): pl.pallas_call(output_kernel, out_shape=(*big, *flat, *big, *flat), in_sp...  1.03 us

profile of v2, /device:TPU:0, one launch (start us, length us, event | category | flops | bytes accessed | tf_op | source)
XLA Modules:
  0.0 43.0 jit_solution(1599981867617374808)
XLA Ops:
  0.6 41.3 %distill_step.1 = (f32[320,320]{1,0:T(8,128)S(1)}, f32[320,320]{1,0:T(8,128)S(1)}, f32[320]{0:T(512)S(1)}, f32[320]{0:T(512)S(1)}, f32[320]{0:T(512)S(1)}, /*index=5*/f32[320]{0:T(512)S(1)}) custom-call(s32[2]{0:T(128)} %refs_0_.1, f32[160,320]{1,0:T(8,128)} %refs_1_.1, f32[80,320]{1,0:T(8,128)} %refs_2_.1, f32[80,320]{1,0:T(8,128)} %refs_3_.1, ...), custom_call_target="tpu_custom_call" | custom-call | tf_op jit(solution)/shard_map/distill_step/pallas_call | solution.py:745
  41.9 1.0 %output_step.1 = (f32[160,320]{1,0:T(8,128)}, f32[80,320]{1,0:T(8,128)}, f32[80,320]{1,0:T(8,128)}, f32[320]{0:T(512)}, f32[320]{0:T(512)}, /*index=5*/f32[160,3...) custom-call(f32[320,320]{1,0:T(8,128)S(1)} %get-tuple-element.16.grads, ...), custom_call_target="tpu_custom_call" | custom-call | tf_op jit(solution)/shard_map/output_step/pallas_call | solution.py:759

commit v3 on v2

--- a/solution.py
+++ b/solution.py
@@ -197,6 +197,11 @@
     return jnp.concatenate(parts, axis=1)
 
 
+def in_pieces(rows):
+    big = rows * 2 // 5 // 16 * 16
+    return {"a": (0, big), "b": (big, big), "c": (2 * big, rows - 2 * big)}
+
+
 def fused_kernel(n_rep, n_sam, names, *refs):
     r = dict(zip(names, refs))
     f32, bf16 = jnp.float32, jnp.bfloat16
@@ -205,7 +210,7 @@
     sw, so, st, tw, to, tt = (r[k] for k in ("sw", "so", "st", "tw", "to", "tt"))
     sg, sb, tg, tb, x_s, x_t = (r[k] for k in ("sg", "sb", "tg", "tb", "x_s", "x_t"))
     rows_in, rows_out, rows_time = sw.shape[0], so.shape[0], st.shape[0]
-    packed_out = r["s2_a"].shape[1]
+    pieces = in_pieces(rows_in)
     width, tokens = x_s.shape
     per = tokens // n_sam
     lo = width // 128 * 128
@@ -305,24 +310,37 @@
     def push(seg, orel, t, r_at, start=0, count=None):
         count = bufs[seg].shape[1] if count is None else count
         part = bufs[seg].at[peer(orel), pl.ds(start, count)]
-        send(part, part, g_send.at[seg], g_recv.at[seg * 4 + r_at], dp_id(t))
+        send(part, part, g_send.at[seg], g_recv.at[seg * 6 + r_at], dp_id(t))
 
     def landed(seg, r_at, count=1):
-        arrive(bufs[seg].at[pl.ds(0, count)], g_recv.at[seg * 4 + r_at])
+        arrive(bufs[seg].at[pl.ds(0, count)], g_recv.at[seg * 6 + r_at])
+
+    def landed_rows(seg, r_at, count):
+        arrive(bufs[seg].at[0, pl.ds(0, count)], g_recv.at[seg * 6 + r_at])
 
     def open_gather(seg):
-        push(seg, 0, 2, 0)
-        push(seg, 0, 4, 1)
+        c = cut(seg)
+        d = bufs[seg].shape[1] - c
+        push(seg, 0, 2, 0, 0, c)
+        push(seg, 0, 4, 1, c, d)
+        push(seg, 0, 2, 4, c, d)
+        push(seg, 0, 4, 5, 0, c)
         push(seg, 0, 1, 3)
         sent.append((bufs[seg].at[pl.ds(0, 7)], g_send.at[seg]))
 
     def relay(seg):
         c = cut(seg)
-        landed(seg, 0)
+        d = bufs[seg].shape[1] - c
+        landed_rows(seg, 0, c)
         push(seg, 2, 4, 2, 0, c)
-        landed(seg, 1)
-        push(seg, 4, 2, 2, c, bufs[seg].shape[1] - c)
+        landed_rows(seg, 1, d)
+        push(seg, 4, 2, 2, c, d)
+
+    def relay_near(seg):
+        c = cut(seg)
+        landed_rows(seg, 4, bufs[seg].shape[1] - c)
         push(seg, 2, 1, 3)
+        landed_rows(seg, 5, c)
         push(seg, 4, 1, 3)
 
     def relay_far(seg):
@@ -362,11 +380,14 @@
     part_s = jnp.dot(feats, st_b, preferred_element_type=f32)
     part_t = jnp.dot(feats, tt_b, preferred_element_type=f32)
     which = lax.rem(lax.broadcasted_iota(jnp.int32, part_s.shape, 0), SUB)
-    e_part[...] = jnp.where(which < n_sam, part_s, part_t).reshape(e_part.shape)
+    part = jnp.where(which < n_sam, part_s, part_t)
+    for d in range(8):
+        put_packed(e_part.at[d], part[d * SUB : d * SUB + 2 * n_sam])
     e_in[pl.ds(me, 1)] = e_part[pl.ds(me, 1)]
     exchange("e", lambda t: e_part.at[peer(t)], lambda t: e_in.at[me], near, dp_id)
     relay(s_in)
     open_gather(out)
+    open_gather(t_out)
 
     ft_all, em_all = r["ft_all"], r["em_all"]
     ft_all[pl.ds(rep, 1)] = jnp.concatenate([tf_all[d, :n_sam, :] for d in range(8)], axis=0).astype(bf16)[None]
@@ -378,14 +399,14 @@
         e_all[start : start + count, :] = ema_decay * target[...] + (1.0 - ema_decay) * student[...]
         start += count
     relay(t_in)
-    open_gather(t_out)
+    relay_near(s_in)
     loaded("x_s", "sg", "sb")
-    relay_far(s_in)
 
     arrive(e_in.at[pl.ds(0, 7)], r["e_recv"])
     emb = e_in[0]
     for k in range(1, 8):
         emb = emb + e_in[k]
+    emb = unpacked(emb, 2 * n_sam, width)
 
     y_v, normed_v, inv_v, nb_v, nbt_v = (r[k] for k in ("y_v", "normed_v", "inv_v", "nb_v", "nbt_v"))
     hid_v, hidt_v, a_v, b_v, gyb_v, gm_v = (r[k] for k in ("hid_v", "hidt_v", "a_v", "b_v", "gyb_v", "gm_v"))
@@ -402,6 +423,9 @@
         summed, inv, normed, nb = normalise(x_s, k, emb[k : k + 1], sg[...][None], sb[...][None])
         y_v[at, :], normed_v[at, :], nb_v[at, :] = summed, normed, nb
         inv_v[at, :] = inv
+    relay_far(s_in)
+    relay(out)
+    relay_near(t_in)
     loaded("x_t", "tg", "tb")
     for k in range(n_sam):
         at = pl.ds(k * per, per)
@@ -409,9 +433,10 @@
             x_t, k, emb[n_sam + k : n_sam + k + 1], tg[...][None], tb[...][None]
         )
         y_v[at, :], nbt_v[at, :] = y_v[at, :] - summed, nb
-    relay(out)
+    relay_near(out)
     close_gather(s_in)
     place_in(s_in, ws_all)
+    relay(t_out)
 
     for k in range(n_sam):
         at = pl.ds(k * per, per)
@@ -425,7 +450,7 @@
         hid_v[at, :] = (act * up).astype(bf16)
         if k == 0:
             relay_far(t_in)
-    relay(t_out)
+            relay_near(t_out)
     relay_far(out)
     close_gather(t_in)
     place_in(t_in, wt_all)
@@ -434,9 +459,10 @@
         gate = contract_last(nbt_v[at, :], wt_all[:ff, :])
         up = contract_last(nbt_v[at, :], wt_all[ff:, :])
         hidt_v[at, :] = (gelu_tanh(gate) * up).astype(bf16)
+        if k == 0:
+            relay_far(t_out)
     close_gather(out)
     place_out(out, os_all, 0)
-    relay_far(t_out)
     for k in range(n_sam):
         at = pl.ds(k * per, per)
         y_v[at, :] = y_v[at, :] + jnp.dot(hid_v[at, :], os_all[...], preferred_element_type=f32)
@@ -448,21 +474,16 @@
         y_v[at, :], gyb_v[at, :] = gy, gy.astype(bf16)
 
     r1_o, r1_i = r["r1_o"], r["r1_i"]
-    blocks = {
-        "o": (r["gs_o"], r1_o, rows_out, 0),
-        "a": (r["gs_i"], r1_i, rows_in, 0),
-        "b": (r["gs_i"], r1_i, rows_in, rows_out),
-    }
 
     def to_core(src, dst, count, q, key):
         part = src.at[pl.ds(pl.multiple_of((2 * q + 1 - core) * count, 16), count)]
         send(part, dst.at[q], r[key + "_send"], r[key + "_recv"], dp_id(1))
 
     def pair(key, rel):
-        g, r1, count, first = blocks[key]
+        first, count = pieces[key]
         owner = peer(rel)
-        own = g[pl.ds(pl.multiple_of(owner * count + first, 16), rows_out), :]
-        return own + r1[lax.div(owner, 2), first : first + rows_out, :].astype(f32)
+        own = r["gs_i"][pl.ds(pl.multiple_of(owner * rows_in + first, 16), count), :]
+        return own + r1_i[lax.div(owner, 2), first : first + count, :].astype(f32)
 
     def to_chip(key, k):
         s2, r2 = r["s2_" + key], r["r2_" + key]
@@ -474,7 +495,6 @@
     r["gb_o"][...] = total_out.astype(bf16)
     for q in range(4):
         to_core(r["gb_o"], r1_o, rows_out, q, "c0")
-
     for k in range(n_sam):
         at = pl.ds(k * per, per)
         gh = contract_last(gyb_v[at, :], os_all[...])
@@ -510,25 +530,28 @@
 
     weight_grad(0)
     arrive(r1_o, r["c0_recv"])
-    z_v, zb_v, rz_v = r["z_v"], r["zb_v"], r["rz_v"]
-    share = rz_v.shape[2]
+    pk_v, z_v, zb_v, rz_v = r["pk_v"], r["z_v"], r["zb_v"], r["rz_v"]
+    share = pk_v.shape[0] // n_rep
     for q in range(4):
         own = r["gs_o"][pl.ds(pl.multiple_of((2 * q + core) * rows_out, 16), rows_out), :]
-        put_packed(z_v.at[q], own + r1_o[q].astype(f32))
-        z_v[q, packed_out:, :] = jnp.zeros((z_v.shape[1] - packed_out, 128), f32)
+        put_packed(pk_v, own + r1_o[q].astype(f32))
         for j in range(n_rep):
-            zb_v[j, q] = z_v[q, j * share : (j + 1) * share, :].astype(bf16)
+            z_v[j, q * share : (q + 1) * share, :] = pk_v[j * share : (j + 1) * share, :]
+    for j in range(n_rep):
+        zb_v[j] = z_v[j].astype(bf16)
     exchange("rz", lambda j: zb_v.at[rep_peer(j)], lambda j: rz_v.at[j], far, rep_id)
     weight_grad(1)
+    arrive(r1_i.at[pl.ds(0, 2)], r["c1_recv"])
+    to_chip("a", 3)
+    to_chip("a", 2)
     for k in range(n_sam):
         more_gain, more_bias = input_grad(k)
         grad_gain, grad_bias = grad_gain + more_gain, grad_bias + more_bias
         if k == 0:
-            arrive(r1_i.at[pl.ds(0, 2)], r["c1_recv"])
-            to_chip("a", 3)
-            to_chip("a", 2)
-    arrive(r1_i.at[pl.ds(0, 2)], r["c2_recv"])
-    to_chip("a", 1)
+            arrive(r1_i.at[pl.ds(0, 2)], r["c2_recv"])
+            to_chip("a", 1)
+            for q in (3, 2, 1):
+                to_chip("b", q)
     high = [v.astype(bf16).astype(f32) for v in (grad_gain, grad_bias)]
     low = [v - h for v, h in zip((grad_gain, grad_bias), high)]
     n_small = n_sam + 4
@@ -537,29 +560,40 @@
     small[pl.ds(me, 1)] = r["pack_v"][...].astype(bf16)[None]
     exchange("sm", lambda t: small.at[me], lambda t: small.at[me], near, dp_id)
     for k in (3, 2, 1):
-        to_chip("b", k)
-    for key in "ab":
+        to_chip("c", k)
+    for key in "abc":
         put_packed(r["p_" + key], pair(key, 0))
 
+    def chips_total(key):
+        p, r2 = r["p_" + key], r["r2_" + key]
+        arrive(r2.at[pl.ds(1, 3)], r["r2r_" + key])
+        p[...] = p[...] + r2[1].astype(f32) + r2[2].astype(f32) + r2[3].astype(f32)
+        return p
+
     def to_planes(key):
-        p, pb, r2, r3 = r["p_" + key], r["pb_" + key], r["r2_" + key], r["r3_" + key]
-        used, share = r2.shape[1], pb.shape[1]
-        arrive(r2.at[pl.ds(1, 3)], r["r2r_" + key])
-        p[:used, :] = p[:used, :] + r2[1].astype(f32) + r2[2].astype(f32) + r2[3].astype(f32)
-        p[used:, :] = jnp.zeros((p.shape[0] - used, 128), f32)
+        p, pb, r3 = chips_total(key), r["pb_" + key], r["r3_" + key]
+        part = pb.shape[1]
         for q in range(n_rep):
-            pb[q] = p[q * share : (q + 1) * share, :].astype(bf16)
+            pb[q] = p[q * part : (q + 1) * part, :].astype(bf16)
         for j in far:
             send(pb.at[rep_peer(j)], r3.at[j], r["r3s_" + key], r["r3r_" + key], rep_id(j))
+
+    def to_planes_whole(key):
+        r3 = r["r3_" + key]
+        r3[pl.ds(rep, 1)] = chips_total(key)[...].astype(bf16)[None]
+        for j in far:
+            send(r3.at[rep], r3.at[rep], r["r3s_" + key], r["r3r_" + key], rep_id(j))
 
     def plane_total():
         arrive(rz_v.at[pl.ds(1, 3)], r["rz_recv"])
         tz_v, tzb_v = r["tz_v"], r["tzb_v"]
+        total = z_v[rep]
+        for j in range(1, n_rep):
+            total = total + rz_v[j].astype(f32)
+        pk_v[...] = total
         for q in range(4):
-            total = z_v[q, pl.ds(pl.multiple_of(rep * share, 8), share), :]
-            for j in range(1, n_rep):
-                total = total + rz_v[j, q].astype(f32)
-            tz_v[q], tzb_v[q] = total, total.astype(bf16)
+            part = pk_v[q * share : (q + 1) * share, :]
+            tz_v[q], tzb_v[q] = part, part.astype(bf16)
         exchange(
             "r2z", lambda k: tzb_v.at[lax.div(peer(2 * k), 2)], lambda k: r["r2z_v"].at[k], (3, 1, 2),
             lambda k: dp_id(2 * k),
@@ -579,9 +613,9 @@
             send(fin.at[rep], fin.at[rep], r["r4s_" + key], r["r4r_" + key], rep_id(j))
 
     def share_total(key):
-        p, r3, fin = r["p_" + key], r["r3_" + key], r["fin_" + key]
-        share = fin.shape[1]
-        total = p[pl.ds(pl.multiple_of(rep * share, 8), share), :]
+        p, r3 = r["p_" + key], r["r3_" + key]
+        part = r3.shape[1]
+        total = p[pl.ds(pl.multiple_of(rep * part, 8), part), :]
         arrive(r3.at[pl.ds(1, 3)], r["r3r_" + key])
         for j in range(1, n_rep):
             total = total + r3[j].astype(f32)
@@ -592,20 +626,28 @@
         g_all[at, :] = grad
         e_all[at, :] = e_all[at, :] - (1.0 - ema_decay) * learn_rate * grad
 
-    def collect(key, start):
-        p, fin = r["p_" + key], r["fin_" + key]
-        share = fin.shape[1]
+    def collect(key, start, count):
+        p, fin = (pk_v if key == "o" else r["p_" + key]), r["fin_" + key]
+        part = fin.shape[1]
         arrive(fin.at[pl.ds(0, 3)], r["r4r_" + key])
         for q in range(n_rep):
-            p[q * share : (q + 1) * share, :] = fin[q].astype(f32)
-        finish(start, unpacked(p[...], rows_out, width))
+            p[q * part : (q + 1) * part, :] = fin[q].astype(f32)
+        finish(start, unpacked(p[...], count, width))
+
+    def collect_whole(key):
+        r3 = r["r3_" + key]
+        arrive(r3.at[pl.ds(0, 3)], r["r3r_" + key])
+        total = r3[0].astype(f32)
+        for j in range(1, n_rep):
+            total = total + r3[j].astype(f32)
+        first, count = pieces[key]
+        finish(first, unpacked(total, count, width))
 
     to_planes("a")
+    to_planes("b")
     arrive(small.at[pl.ds(0, 7)], r["sm_recv"])
     part = [small[d].astype(f32) for d in range(8)]
-    em_all[pl.ds(rep, 1)] = jnp.concatenate(
-        [unpacked(p, n_small, width)[:n_sam] for p in part], axis=0
-    ).astype(bf16)[None]
+    put_packed(em_all.at[rep], jnp.concatenate([unpacked(p, n_small, width)[:n_sam] for p in part], axis=0))
     sums = part[0]
     for k in range(1, 8):
         sums = sums + part[k]
@@ -617,34 +659,36 @@
     exchange("em", lambda j: em_all.at[rep], lambda j: em_all.at[rep], far, rep_id)
     exchange("rs", lambda j: small_rep.at[rep], lambda j: small_rep.at[rep], far, rep_id)
     plane_total()
-    to_planes("b")
+    to_planes_whole("c")
     share_total("a")
     chip_total()
+    share_total("b")
+    collect_whole("c")
     arrive(ft_all.at[pl.ds(0, 3)], r["ft_recv"])
     arrive(em_all.at[pl.ds(0, 3)], r["em_recv"])
     arrive(small_rep.at[pl.ds(0, 3)], r["rs_recv"])
-    grad_time = contract_first(ft_all[0], em_all[0])
+    grad_time = jnp.zeros((rows_time, width), f32)
+    for j in range(n_rep):
+        samples = unpacked(em_all[j].astype(f32), 8 * n_sam, width).astype(bf16)
+        grad_time = grad_time + contract_first(ft_all[j], samples)
     sums = jnp.zeros((2, width), f32)
     for j in range(n_rep):
         part = unpacked(small_rep[j].astype(f32), 4, width)
         sums = sums + part[:2] + part[2:]
-    for j in range(1, n_rep):
-        grad_time = grad_time + contract_first(ft_all[j], em_all[j])
     finish(rows_in + rows_out, grad_time)
     gg, gb = sums[0, :], sums[1, :]
     r["gg_o"][...], r["gb_o_"][...] = gg, gb
     r["eg_o"][...] = average(tg[...], sg[...], gg)
     r["eb_o"][...] = average(tb[...], sb[...], gb)
-    share_total("b")
-    collect("o", rows_in)
-    collect("a", 0)
-    collect("b", rows_out)
+    collect("a", *pieces["a"])
+    collect("o", rows_in, rows_out)
+    collect("b", *pieces["b"])
     for key, ref in (("tf", tf_all), ("e", e_in), ("sm", small)):
         sent.append((ref.at[pl.ds(0, 7)], r[key + "_send"]))
     for key, ref in (("ft", ft_all), ("em", em_all), ("rs", small_rep)):
         sent.append((ref.at[pl.ds(0, 3)], r[key + "_send"]))
     sent += [(r1_o, r["c0_send"]), (r1_i.at[pl.ds(0, 2)], r["c1_send"]), (r1_i.at[pl.ds(0, 2)], r["c2_send"])]
-    for key in "ab":
+    for key in "abc":
         sent.append((r["r2_" + key].at[pl.ds(0, 3)], r["r2s_" + key]))
         sent.append((r["r3_" + key].at[pl.ds(0, 3)], r["r3s_" + key]))
     sent += [(rz_v.at[pl.ds(0, 3)], r["rz_send"]), (r["r2z_v"].at[pl.ds(0, 3)], r["r2z_send"])]
@@ -687,9 +731,9 @@
     vm = pltpu.VMEM
     dma = pltpu.SemaphoreType.DMA
     full = width // 128
+    rows_emb = -(-(2 * n_sam * full + n_sam) // SUB) * SUB
     rows_small = -(-((n_sam + 4) * full + (n_sam + 4) // 2) // 16) * 16
     packed_in, packed_out = rows_in * full + rows_in // 2, rows_out * full + rows_out // 2
-    share = -(-packed_out // (8 * n_rep)) * 8
     scratch = dict(
         ts=pltpu.SMEM((n_sam,), jnp.int32),
         sw=vm(sw.shape, f32), so=vm(so.shape, f32), st=vm(st.shape, f32),
@@ -701,9 +745,9 @@
         ws_all=vm((n_dp * rows_in, width), bf16), os_all=vm((ff, width), bf16),
         wt_all=vm((n_dp * rows_in, width), bf16), ot_all=vm((ff, width), bf16),
         tf_own=vm((n_dp, SUB, rows_time), f32), tf_all=vm((n_dp, SUB, rows_time), f32),
-        e_part=vm((n_dp, SUB, width), f32), e_in=vm((n_dp, SUB, width), f32),
+        e_part=vm((n_dp, rows_emb, 128), f32), e_in=vm((n_dp, rows_emb, 128), f32),
         small=vm((n_dp, rows_small, 128), bf16), pack_v=vm((rows_small, 128), f32), small_rep=vm((n_rep, rows_small, 128), bf16),
-        ft_all=vm((n_rep, n_dp * n_sam, rows_time), bf16), em_all=vm((n_rep, n_dp * n_sam, width), bf16),
+        ft_all=vm((n_rep, n_dp * n_sam, rows_time), bf16), em_all=vm((n_rep, n_dp * n_sam * full + n_dp * n_sam // 2, 128), bf16),
         normed_v=vm((tokens, width), f32), inv_v=vm((tokens, 1), f32), nb_v=vm((tokens, width), bf16),
         hid_v=vm((tokens, ff), bf16), hidt_v=vm((tokens, ff), bf16), a_v=vm((tokens, ff), f32), b_v=vm((tokens, ff), f32),
         y_v=vm((tokens, width), f32), nbt_v=vm((tokens, width), bf16), gyb_v=vm((tokens, width), bf16),
@@ -711,25 +755,28 @@
         gs_i=vm((n_dp * rows_in, width), f32), gs_o=vm((ff, width), f32),
         gb_i=vm((n_dp * rows_in, width), bf16), gb_o=vm((ff, width), bf16),
         r1_i=vm((4, rows_in, width), bf16), r1_o=vm((4, rows_out, width), bf16),
-        ld_sem=dma((len(LOADED),)), g_send=dma((4,)), g_recv=dma((16,)),
-    )
-    for key in "oab":
-        scratch["p_" + key] = vm((n_rep * share, 128), f32)
-        scratch["fin_" + key] = vm((n_rep, share, 128), bf16)
-        scratch["r4s_" + key], scratch["r4r_" + key] = dma, dma
-    for key in "ab":
+        ld_sem=dma((len(LOADED),)), g_send=dma((4,)), g_recv=dma((24,)),
+    )
+    for key, (_, count) in in_pieces(rows_in).items():
+        packed = count * full + count // 2
+        scratch["p_" + key] = vm((packed, 128), f32)
         for name in ("s2_", "r2_"):
-            scratch[name + key] = vm((4, packed_out, 128), bf16)
-        for name in ("pb_", "r3_"):
-            scratch[name + key] = vm((n_rep, share, 128), bf16)
+            scratch[name + key] = vm((4, packed, 128), bf16)
+        scratch["r3_" + key] = vm((n_rep, packed if key == "c" else packed // n_rep, 128), bf16)
+        if key != "c":
+            scratch["pb_" + key] = vm((n_rep, packed // n_rep, 128), bf16)
         for name in ("r2", "r3"):
             scratch[name + "s_" + key], scratch[name + "r_" + key] = dma, dma
-    scratch["z_v"] = vm((4, n_rep * share, 128), f32)
+    for key, packed in (("a", scratch["p_a"].shape[0]), ("b", scratch["p_b"].shape[0]), ("o", packed_out)):
+        scratch["fin_" + key] = vm((n_rep, packed // n_rep, 128), bf16)
+        scratch["r4s_" + key], scratch["r4r_" + key] = dma, dma
+    scratch["pk_v"] = vm((packed_out, 128), f32)
+    scratch["z_v"] = vm((n_rep, packed_out, 128), f32)
     for name in ("zb_v", "rz_v"):
-        scratch[name] = vm((n_rep, 4, share, 128), bf16)
-    scratch["tz_v"] = vm((4, share, 128), f32)
+        scratch[name] = vm((n_rep, packed_out, 128), bf16)
+    scratch["tz_v"] = vm((4, packed_out // n_rep, 128), f32)
     for name in ("tzb_v", "r2z_v"):
-        scratch[name] = vm((4, share, 128), bf16)
+        scratch[name] = vm((4, packed_out // n_rep, 128), bf16)
     for key in ("tf", "e", "sm", "ft", "em", "rs", "c0", "c1", "c2", "rz", "r2z"):
         scratch[key + "_send"], scratch[key + "_recv"] = dma, dma
     shape = jax.ShapeDtypeStruct
@@ -782,6 +829,8 @@
         and (tokens // samples) % 128 == 0
         and all(r % (16 * n_dp) == 0 for r in rows)
         and all(r % (32 * n_dp) == 0 for r in rows[:1])
+        and in_pieces(rows[0] // n_dp)["a"][1] % 64 == 0
+        and in_pieces(rows[0] // n_dp)["a"][1] > 0
         and rows[0] == 2 * rows[1]
         and rows[2] == rows[1]
         and args[0].shape[1] % 128 == 64

time: 43.1 us -> 41.9 us (0.972)
  Pallas kernels: 42.3 us -> 41 us
    pallas_call x1, Pallas kernels: 41.3 us -> 40 us  [fused_device(): pl.pallas_call(functools.partial(fused_kernel, n_rep, n_sam, names), out_...]
where the time goes in v3:
time: 41.9 us; the launch traced here: 41.7 us
  Pallas kernels  41 us (98%)
  between operations  0.66 us (2%)
    pallas_call x1, Pallas kernels, fused_device(): pl.pallas_call(functools.partial(fused_kernel, n_rep, n_sam, names), out_...  40 us
    pallas_call x1, Pallas kernels, fused_device(): pl.pallas_call(output_kernel, out_shape=(*big, *flat, *big, *flat), in_sp...  1.03 us

profile of v3, /device:TPU:0, one launch (start us, length us, event | category | flops | bytes accessed | tf_op | source)
XLA Modules:
  0.0 41.7 jit_solution(16725071538038510929)
XLA Ops:
  0.6 40.0 %distill_step.1 = (f32[320,320]{1,0:T(8,128)S(1)}, f32[320,320]{1,0:T(8,128)S(1)}, f32[320]{0:T(512)S(1)}, f32[320]{0:T(512)S(1)}, f32[320]{0:T(512)S(1)}, /*index=5*/f32[320]{0:T(512)S(1)}) custom-call(s32[2]{0:T(128)} %refs_0_.1, f32[160,320]{1,0:T(8,128)} %refs_1_.1, f32[80,320]{1,0:T(8,128)} %refs_2_.1, f32[80,320]{1,0:T(8,128)} %refs_3_.1, ...), custom_call_target="tpu_custom_call" | custom-call | tf_op jit(solution)/shard_map/distill_step/pallas_call | solution.py:792
  40.7 1.0 %output_step.1 = (f32[160,320]{1,0:T(8,128)}, f32[80,320]{1,0:T(8,128)}, f32[80,320]{1,0:T(8,128)}, f32[320]{0:T(512)}, f32[320]{0:T(512)}, /*index=5*/f32[160,3...) custom-call(f32[320,320]{1,0:T(8,128)S(1)} %get-tuple-element.16.grads, ...), custom_call_target="tpu_custom_call" | custom-call | tf_op jit(solution)/shard_map/output_step/pallas_call | solution.py:806

commit v4 on v3

--- a/solution.py
+++ b/solution.py
@@ -237,8 +237,12 @@
     barrier = pltpu.get_barrier_semaphore()
     for t in range(1, 8):
         pl.semaphore_signal(barrier, inc=1, device_id=dp_id(t), device_id_type=MESH)
-    for j in range(1, n_rep):
-        pl.semaphore_signal(barrier, inc=1, device_id=rep_id(j), device_id_type=MESH)
+    for valid, step in ((rep > 0, -1), (rep < n_rep - 1, 1)):
+
+        @pl.when(valid)
+        def _(step=step):
+            pl.semaphore_signal(barrier, inc=1, device_id={"rep": rep + step}, device_id_type=MESH)
+
 
     loads = []
     for i, name in enumerate(LOADED):
@@ -292,6 +296,80 @@
     tf_all[pl.ds(me, 1)] = tf_own[pl.ds(me, 1)]
     loaded("sw")
     put_packed(bufs[s_in].at[me], sw[...])
+    pl.semaphore_wait(barrier, 7 + jnp.minimum(rep, 1) + jnp.minimum(n_rep - 1 - rep, 1))
+
+    def cut(seg):
+        return bufs[seg].shape[1] // 32 * 16
+
+    def push(seg, orel, t, r_at, start=0, count=None):
+        count = bufs[seg].shape[1] if count is None else count
+        part = bufs[seg].at[peer(orel), pl.ds(start, count)]
+        send(part, part, g_send.at[seg], g_recv.at[seg * 5 + r_at], dp_id(t))
+
+    def landed(seg, r_at, count=1):
+        arrive(bufs[seg].at[pl.ds(0, count)], g_recv.at[seg * 5 + r_at])
+
+    def landed_rows(seg, r_at, count):
+        arrive(bufs[seg].at[0, pl.ds(0, count)], g_recv.at[seg * 5 + r_at])
+
+    def open_gather(seg):
+        c = cut(seg)
+        d = bufs[seg].shape[1] - c
+        push(seg, 0, 2, 0, 0, c)
+        push(seg, 0, 4, 1, c, d)
+        push(seg, 0, 2, 4, c, d)
+        push(seg, 0, 4, 4, 0, c)
+        push(seg, 0, 1, 3)
+        sent.append((bufs[seg].at[pl.ds(0, 7)], g_send.at[seg]))
+
+    def relay(seg):
+        c = cut(seg)
+        d = bufs[seg].shape[1] - c
+        landed_rows(seg, 0, c)
+        push(seg, 2, 4, 2, 0, c)
+        landed_rows(seg, 1, d)
+        push(seg, 4, 2, 2, c, d)
+
+    def relay_near(seg):
+        landed(seg, 4)
+        push(seg, 2, 1, 3)
+        push(seg, 4, 1, 3)
+
+    def relay_far(seg):
+        landed(seg, 2)
+        push(seg, 6, 1, 3)
+
+    def close_gather(seg):
+        landed(seg, 3, 4)
+
+    here, there = (0, 2, 4, 6), (1, 3, 5, 7)
+
+    def place_in(seg, dst, rels):
+        half = rows_in // 2
+        at = lo // 128 * rows_in
+        for o in map(peer, rels):
+            first = pl.multiple_of(o * rows_in, 16)
+            second = pl.multiple_of(o * rows_in + half, 16)
+            for i in range(lo // 128):
+                dst[pl.ds(first, rows_in), i * 128 : (i + 1) * 128] = bufs[seg][o, i * rows_in : (i + 1) * rows_in, :]
+            tail = bufs[seg][o, at : at + half, :]
+            dst[pl.ds(first, half), lo:] = tail[:, :rest]
+            dst[pl.ds(second, half), lo:] = tail[:, rest:]
+
+    def place_out(seg, dst, lanes, rels):
+        at = lo // 128 * rows_out
+        for o in map(peer, rels):
+            first = pl.multiple_of(o * rows_out, 16)
+            for i in range(lo // 128):
+                dst[pl.ds(first, rows_out), i * 128 : (i + 1) * 128] = bufs[seg][o, i * rows_out : (i + 1) * rows_out, :]
+            dst[pl.ds(first, rows_out), lo:] = bufs[out][o, at : at + rows_out, :][:, lanes : lanes + rest]
+
+    near = (1, 2, 4, 3, 5, 6, 7)
+    exchange("tf", lambda t: tf_own.at[peer(t)], lambda t: tf_all.at[me], near, dp_id)
+    open_gather(s_in)
+    loaded("tw")
+    put_packed(bufs[t_in].at[me], tw[...])
+    open_gather(t_in)
     loaded("so", "to")
     for i in range(lo // 128):
         at, lanes = slice(i * rows_out, (i + 1) * rows_out), slice(i * 128, (i + 1) * 128)
@@ -299,81 +377,7 @@
         bufs[t_out][me, at, :] = to[:, lanes].astype(bf16)
     at = slice(lo // 128 * rows_out, (lo // 128 + 1) * rows_out)
     bufs[out][me, at, :] = jnp.concatenate([so[:, lo:], to[:, lo:]], axis=1).astype(bf16)
-    loaded("tw")
-    put_packed(bufs[t_in].at[me], tw[...])
     loaded("st", "tt")
-    pl.semaphore_wait(barrier, 7 + n_rep - 1)
-
-    def cut(seg):
-        return bufs[seg].shape[1] // 32 * 16
-
-    def push(seg, orel, t, r_at, start=0, count=None):
-        count = bufs[seg].shape[1] if count is None else count
-        part = bufs[seg].at[peer(orel), pl.ds(start, count)]
-        send(part, part, g_send.at[seg], g_recv.at[seg * 6 + r_at], dp_id(t))
-
-    def landed(seg, r_at, count=1):
-        arrive(bufs[seg].at[pl.ds(0, count)], g_recv.at[seg * 6 + r_at])
-
-    def landed_rows(seg, r_at, count):
-        arrive(bufs[seg].at[0, pl.ds(0, count)], g_recv.at[seg * 6 + r_at])
-
-    def open_gather(seg):
-        c = cut(seg)
-        d = bufs[seg].shape[1] - c
-        push(seg, 0, 2, 0, 0, c)
-        push(seg, 0, 4, 1, c, d)
-        push(seg, 0, 2, 4, c, d)
-        push(seg, 0, 4, 5, 0, c)
-        push(seg, 0, 1, 3)
-        sent.append((bufs[seg].at[pl.ds(0, 7)], g_send.at[seg]))
-
-    def relay(seg):
-        c = cut(seg)
-        d = bufs[seg].shape[1] - c
-        landed_rows(seg, 0, c)
-        push(seg, 2, 4, 2, 0, c)
-        landed_rows(seg, 1, d)
-        push(seg, 4, 2, 2, c, d)
-
-    def relay_near(seg):
-        c = cut(seg)
-        landed_rows(seg, 4, bufs[seg].shape[1] - c)
-        push(seg, 2, 1, 3)
-        landed_rows(seg, 5, c)
-        push(seg, 4, 1, 3)
-
-    def relay_far(seg):
-        landed(seg, 2)
-        push(seg, 6, 1, 3)
-
-    def close_gather(seg):
-        landed(seg, 3, 4)
-
-    def place_in(seg, dst):
-        half = rows_in // 2
-        for o in range(8):
-            for i in range(lo // 128):
-                dst[o * rows_in : (o + 1) * rows_in, i * 128 : (i + 1) * 128] = bufs[seg][
-                    o, i * rows_in : (i + 1) * rows_in, :
-                ]
-            at = lo // 128 * rows_in
-            tail = bufs[seg][o, at : at + half, :]
-            dst[o * rows_in : o * rows_in + half, lo:] = tail[:, :rest]
-            dst[o * rows_in + half : (o + 1) * rows_in, lo:] = tail[:, rest:]
-
-    def place_out(seg, dst, first):
-        for o in range(8):
-            to_rows = slice(o * rows_out, (o + 1) * rows_out)
-            for i in range(lo // 128):
-                dst[to_rows, i * 128 : (i + 1) * 128] = bufs[seg][o, i * rows_out : (i + 1) * rows_out, :]
-            at = lo // 128 * rows_out
-            dst[to_rows, lo:] = bufs[out][o, at : at + rows_out, :][:, first : first + rest]
-
-    near = (1, 2, 4, 3, 5, 6, 7)
-    exchange("tf", lambda t: tf_own.at[peer(t)], lambda t: tf_all.at[me], near, dp_id)
-    open_gather(s_in)
-    open_gather(t_in)
     st_b, tt_b = st[...].astype(bf16), tt[...].astype(bf16)
     arrive(tf_all.at[pl.ds(0, 7)], r["tf_recv"])
     feats = tf_all[...].reshape(8 * SUB, rows_time).astype(bf16)
@@ -392,15 +396,47 @@
     ft_all, em_all = r["ft_all"], r["em_all"]
     ft_all[pl.ds(rep, 1)] = jnp.concatenate([tf_all[d, :n_sam, :] for d in range(8)], axis=0).astype(bf16)[None]
     far = (3, 2, 1)
-    exchange("ft", lambda j: ft_all.at[rep], lambda j: ft_all.at[rep], far, rep_id)
+
+    def pass_features(hops):
+        for back, valid, onward in ((-1, rep >= hops, rep < n_rep - 1), (1, rep + hops < n_rep, rep > 0)):
+
+            @pl.when(valid)
+            def _(back=back, onward=onward):
+                b = rep + back * hops
+                at = ft_all.at[b]
+                if hops:
+                    arrive(at, r["ft_recv"].at[b])
+
+                @pl.when(onward)
+                def _():
+                    send(at, at, r["ft_send"].at[(1 + back) // 2], r["ft_recv"].at[b], {"rep": rep - back})
+
+    def features_sent():
+        for k in range(n_rep):
+
+            @pl.when(rep == k)
+            def _(k=k):
+                if k < n_rep - 1:
+                    bytes_of(ft_all.at[pl.ds(0, k + 1)], r["ft_send"].at[0]).wait_send()
+                if k > 0:
+                    bytes_of(ft_all.at[pl.ds(0, n_rep - k)], r["ft_send"].at[1]).wait_send()
+
+    pass_features(0)
     start = 0
     for student, target in ((sw, tw), (so, to), (st, tt)):
         count = student.shape[0]
         e_all[start : start + count, :] = ema_decay * target[...] + (1.0 - ema_decay) * student[...]
         start += count
+    y_v, normed_v, inv_v, nb_v, nbt_v = (r[k] for k in ("y_v", "normed_v", "inv_v", "nb_v", "nbt_v"))
+    xt_v = r["xt_v"]
+    loaded("x_s", "sg", "sb")
+    for k in range(n_sam):
+        y_v[pl.ds(k * per, per), :] = x_s[:, pl.ds(k * per, per)].astype(f32).T
     relay(t_in)
     relay_near(s_in)
-    loaded("x_s", "sg", "sb")
+    loaded("x_t", "tg", "tb")
+    for k in range(n_sam):
+        xt_v[pl.ds(k * per, per), :] = x_t[:, pl.ds(k * per, per)].astype(f32).T
 
     arrive(e_in.at[pl.ds(0, 7)], r["e_recv"])
     emb = e_in[0]
@@ -408,11 +444,10 @@
         emb = emb + e_in[k]
     emb = unpacked(emb, 2 * n_sam, width)
 
-    y_v, normed_v, inv_v, nb_v, nbt_v = (r[k] for k in ("y_v", "normed_v", "inv_v", "nb_v", "nbt_v"))
     hid_v, hidt_v, a_v, b_v, gyb_v, gm_v = (r[k] for k in ("hid_v", "hidt_v", "a_v", "b_v", "gyb_v", "gm_v"))
 
-    def normalise(x_ref, k, shift, gain, bias):
-        summed = x_ref[:, pl.ds(k * per, per)].astype(f32).T + shift
+    def normalise(x_rows, k, shift, gain, bias):
+        summed = x_rows[pl.ds(k * per, per), :] + shift
         center = summed - jnp.mean(summed, axis=1, keepdims=True)
         inv = lax.rsqrt(jnp.mean(center * center, axis=1, keepdims=True) + 1e-05)
         normed = center * inv
@@ -420,59 +455,66 @@
 
     for k in range(n_sam):
         at = pl.ds(k * per, per)
-        summed, inv, normed, nb = normalise(x_s, k, emb[k : k + 1], sg[...][None], sb[...][None])
+        summed, inv, normed, nb = normalise(y_v, k, emb[k : k + 1], sg[...][None], sb[...][None])
         y_v[at, :], normed_v[at, :], nb_v[at, :] = summed, normed, nb
         inv_v[at, :] = inv
     relay_far(s_in)
     relay(out)
     relay_near(t_in)
-    loaded("x_t", "tg", "tb")
     for k in range(n_sam):
         at = pl.ds(k * per, per)
         summed, inv, normed, nb = normalise(
-            x_t, k, emb[n_sam + k : n_sam + k + 1], tg[...][None], tb[...][None]
+            xt_v, k, emb[n_sam + k : n_sam + k + 1], tg[...][None], tb[...][None]
         )
         y_v[at, :], nbt_v[at, :] = y_v[at, :] - summed, nb
+    pass_features(1)
     relay_near(out)
+    place_in(s_in, ws_all, here)
     close_gather(s_in)
-    place_in(s_in, ws_all)
+    place_in(s_in, ws_all, there)
     relay(t_out)
 
     for k in range(n_sam):
         at = pl.ds(k * per, per)
         gate = contract_last(nb_v[at, :], ws_all[:ff, :])
         up = contract_last(nb_v[at, :], ws_all[ff:, :])
-        tangent = jnp.tanh(GATE_C * (gate + 0.044715 * gate * gate * gate))
-        half = 0.5 * (1.0 + tangent)
+        square = gate * gate
+        half = 0.5 + 0.5 * jnp.tanh(gate * (GATE_C + GATE_C * 0.044715 * square))
         act = gate * half
-        slope = half + 0.5 * gate * (1.0 - tangent * tangent) * GATE_C * (1.0 + 0.134145 * gate * gate)
+        slope = half + act * (1.0 - half) * (2.0 * GATE_C + 2.0 * GATE_C * 0.134145 * square)
         a_v[at, :], b_v[at, :] = up * slope, act
         hid_v[at, :] = (act * up).astype(bf16)
         if k == 0:
             relay_far(t_in)
             relay_near(t_out)
     relay_far(out)
+    pass_features(2)
+    place_in(t_in, wt_all, here)
     close_gather(t_in)
-    place_in(t_in, wt_all)
+    place_in(t_in, wt_all, there)
     for k in range(n_sam):
         at = pl.ds(k * per, per)
         gate = contract_last(nbt_v[at, :], wt_all[:ff, :])
         up = contract_last(nbt_v[at, :], wt_all[ff:, :])
-        hidt_v[at, :] = (gelu_tanh(gate) * up).astype(bf16)
+        half = 0.5 + 0.5 * jnp.tanh(gate * (GATE_C + GATE_C * 0.044715 * (gate * gate)))
+        hidt_v[at, :] = (gate * half * up).astype(bf16)
         if k == 0:
             relay_far(t_out)
+    place_out(out, os_all, 0, here)
     close_gather(out)
-    place_out(out, os_all, 0)
+    place_out(out, os_all, 0, there)
     for k in range(n_sam):
         at = pl.ds(k * per, per)
         y_v[at, :] = y_v[at, :] + jnp.dot(hid_v[at, :], os_all[...], preferred_element_type=f32)
+    place_out(t_out, ot_all, rest, here)
     close_gather(t_out)
-    place_out(t_out, ot_all, rest)
+    place_out(t_out, ot_all, rest, there)
     for k in range(n_sam):
         at = pl.ds(k * per, per)
         gy = (y_v[at, :] - jnp.dot(hidt_v[at, :], ot_all[...], preferred_element_type=f32)) * (1.0 / tokens)
         y_v[at, :], gyb_v[at, :] = gy, gy.astype(bf16)
 
+    pass_features(3)
     r1_o, r1_i = r["r1_o"], r["r1_i"]
 
     def to_core(src, dst, count, q, key):
@@ -511,7 +553,7 @@
     grad_gain = jnp.zeros((1, width), f32)
     grad_bias = grad_gain
     embs = []
-    small, small_rep = r["small"], r["small_rep"]
+    small = r["small"]
 
     def input_grad(k):
         at = pl.ds(k * per, per)
@@ -578,11 +620,18 @@
         for j in far:
             send(pb.at[rep_peer(j)], r3.at[j], r["r3s_" + key], r["r3r_" + key], rep_id(j))
 
-    def to_planes_whole(key):
+    def to_next_plane(key):
         r3 = r["r3_" + key]
-        r3[pl.ds(rep, 1)] = chips_total(key)[...].astype(bf16)[None]
-        for j in far:
-            send(r3.at[rep], r3.at[rep], r["r3s_" + key], r["r3r_" + key], rep_id(j))
+        slot = lax.rem(rep, 2)
+        r3[pl.ds(slot, 1)] = chips_total(key)[...].astype(bf16)[None]
+        send(r3.at[slot], r3.at[slot], r["r3s_" + key], r["r3r_" + key], rep_id(1))
+
+    def to_far_plane(key):
+        r3, r4 = r["r3_" + key], r["r4_" + key]
+        slot = lax.div(rep, 2)
+        arrive(r3.at[0], r["r3r_" + key])
+        r4[pl.ds(slot, 1)] = (r3[0].astype(f32) + r3[1].astype(f32)).astype(bf16)[None]
+        send(r4.at[slot], r4.at[slot], r["r4s_" + key], r["r4r_" + key], rep_id(2))
 
     def plane_total():
         arrive(rz_v.at[pl.ds(1, 3)], r["rz_recv"])
@@ -635,19 +684,16 @@
         finish(start, unpacked(p[...], count, width))
 
     def collect_whole(key):
-        r3 = r["r3_" + key]
-        arrive(r3.at[pl.ds(0, 3)], r["r3r_" + key])
-        total = r3[0].astype(f32)
-        for j in range(1, n_rep):
-            total = total + r3[j].astype(f32)
+        r4 = r["r4_" + key]
+        arrive(r4.at[0], r["r4r_" + key])
         first, count = pieces[key]
-        finish(first, unpacked(total, count, width))
+        finish(first, unpacked(r4[0].astype(f32) + r4[1].astype(f32), count, width))
 
     to_planes("a")
     to_planes("b")
+    plane_total()
     arrive(small.at[pl.ds(0, 7)], r["sm_recv"])
     part = [small[d].astype(f32) for d in range(8)]
-    put_packed(em_all.at[rep], jnp.concatenate([unpacked(p, n_small, width)[:n_sam] for p in part], axis=0))
     sums = part[0]
     for k in range(1, 8):
         sums = sums + part[k]
@@ -655,25 +701,39 @@
     sums = sums[n_sam : n_sam + 2] + sums[n_sam + 2 : n_sam + 4]
     high = sums.astype(bf16).astype(f32)
     put_packed(r["pack_v"], jnp.concatenate([high, sums - high], axis=0))
-    small_rep[pl.ds(rep, 1)] = r["pack_v"][...].astype(bf16)[None]
-    exchange("em", lambda j: em_all.at[rep], lambda j: em_all.at[rep], far, rep_id)
-    exchange("rs", lambda j: small_rep.at[rep], lambda j: small_rep.at[rep], far, rep_id)
-    plane_total()
-    to_planes_whole("c")
+    n_em = em_all.shape[1] - small.shape[1]
+    put_packed(em_all.at[rep], jnp.concatenate([unpacked(p, n_small, width)[:n_sam] for p in part], axis=0))
+    em_all[pl.ds(rep, 1), n_em:, :] = r["pack_v"][...].astype(bf16)[None]
+
+    @pl.when(core == 1)
+    def _():
+        exchange("em", lambda j: em_all.at[rep], lambda j: em_all.at[rep], far, rep_id)
+
+    def pass_to_core():
+        arrive(em_all.at[pl.ds(0, 3)], r["em_recv"])
+        for j in far:
+            at = em_all.at[rep_peer(j)]
+            send(at, at, r["rs_send"], r["em_recv"], dp_id(1))
+
+    to_next_plane("c")
     share_total("a")
+    share_total("b")
+    to_far_plane("c")
     chip_total()
-    share_total("b")
+    pl.when(core == 1)(pass_to_core)
     collect_whole("c")
-    arrive(ft_all.at[pl.ds(0, 3)], r["ft_recv"])
-    arrive(em_all.at[pl.ds(0, 3)], r["em_recv"])
-    arrive(small_rep.at[pl.ds(0, 3)], r["rs_recv"])
+
+    @pl.when(core == 0)
+    def _():
+        arrive(em_all.at[pl.ds(0, 3)], r["em_recv"])
+
     grad_time = jnp.zeros((rows_time, width), f32)
     for j in range(n_rep):
-        samples = unpacked(em_all[j].astype(f32), 8 * n_sam, width).astype(bf16)
+        samples = unpacked(em_all[j, :n_em, :].astype(f32), 8 * n_sam, width).astype(bf16)
         grad_time = grad_time + contract_first(ft_all[j], samples)
     sums = jnp.zeros((2, width), f32)
     for j in range(n_rep):
-        part = unpacked(small_rep[j].astype(f32), 4, width)
+        part = unpacked(em_all[j, n_em:, :].astype(f32), 4, width)
         sums = sums + part[:2] + part[2:]
     finish(rows_in + rows_out, grad_time)
     gg, gb = sums[0, :], sums[1, :]
@@ -681,21 +741,26 @@
     r["eg_o"][...] = average(tg[...], sg[...], gg)
     r["eb_o"][...] = average(tb[...], sb[...], gb)
     collect("a", *pieces["a"])
+    collect("b", *pieces["b"])
     collect("o", rows_in, rows_out)
-    collect("b", *pieces["b"])
     for key, ref in (("tf", tf_all), ("e", e_in), ("sm", small)):
         sent.append((ref.at[pl.ds(0, 7)], r[key + "_send"]))
-    for key, ref in (("ft", ft_all), ("em", em_all), ("rs", small_rep)):
-        sent.append((ref.at[pl.ds(0, 3)], r[key + "_send"]))
     sent += [(r1_o, r["c0_send"]), (r1_i.at[pl.ds(0, 2)], r["c1_send"]), (r1_i.at[pl.ds(0, 2)], r["c2_send"])]
     for key in "abc":
         sent.append((r["r2_" + key].at[pl.ds(0, 3)], r["r2s_" + key]))
-        sent.append((r["r3_" + key].at[pl.ds(0, 3)], r["r3s_" + key]))
+        sent.append((r["r3_" + key].at[0] if key == "c" else r["r3_" + key].at[pl.ds(0, 3)], r["r3s_" + key]))
+    sent.append((r["r4_c"].at[0], r["r4s_c"]))
     sent += [(rz_v.at[pl.ds(0, 3)], r["rz_send"]), (r["r2z_v"].at[pl.ds(0, 3)], r["r2z_send"])]
     for key in "oab":
         sent.append((r["fin_" + key].at[pl.ds(0, 3)], r["r4s_" + key]))
     for ref, sem in sent:
         bytes_of(ref, sem).wait_send()
+    features_sent()
+
+    @pl.when(core == 1)
+    def _():
+        for key in ("em_send", "rs_send"):
+            bytes_of(em_all.at[pl.ds(0, 3)], r[key]).wait_send()
 
 
 LOADED = ("ts", "sw", "so", "to", "tw", "st", "tt", "x_s", "sg", "sb", "x_t", "tg", "tb")
@@ -746,24 +811,28 @@
         wt_all=vm((n_dp * rows_in, width), bf16), ot_all=vm((ff, width), bf16),
         tf_own=vm((n_dp, SUB, rows_time), f32), tf_all=vm((n_dp, SUB, rows_time), f32),
         e_part=vm((n_dp, rows_emb, 128), f32), e_in=vm((n_dp, rows_emb, 128), f32),
-        small=vm((n_dp, rows_small, 128), bf16), pack_v=vm((rows_small, 128), f32), small_rep=vm((n_rep, rows_small, 128), bf16),
-        ft_all=vm((n_rep, n_dp * n_sam, rows_time), bf16), em_all=vm((n_rep, n_dp * n_sam * full + n_dp * n_sam // 2, 128), bf16),
+        small=vm((n_dp, rows_small, 128), bf16), pack_v=vm((rows_small, 128), f32),
+        ft_all=vm((n_rep, n_dp * n_sam, rows_time), bf16), em_all=vm((n_rep, n_dp * n_sam * full + n_dp * n_sam // 2 + rows_small, 128), bf16),
         normed_v=vm((tokens, width), f32), inv_v=vm((tokens, 1), f32), nb_v=vm((tokens, width), bf16),
         hid_v=vm((tokens, ff), bf16), hidt_v=vm((tokens, ff), bf16), a_v=vm((tokens, ff), f32), b_v=vm((tokens, ff), f32),
-        y_v=vm((tokens, width), f32), nbt_v=vm((tokens, width), bf16), gyb_v=vm((tokens, width), bf16),
+        y_v=vm((tokens, width), f32), xt_v=vm((tokens, width), f32), nbt_v=vm((tokens, width), bf16), gyb_v=vm((tokens, width), bf16),
         gm_v=vm((2, tokens, ff), bf16),
         gs_i=vm((n_dp * rows_in, width), f32), gs_o=vm((ff, width), f32),
         gb_i=vm((n_dp * rows_in, width), bf16), gb_o=vm((ff, width), bf16),
         r1_i=vm((4, rows_in, width), bf16), r1_o=vm((4, rows_out, width), bf16),
-        ld_sem=dma((len(LOADED),)), g_send=dma((4,)), g_recv=dma((24,)),
+        rs_send=dma, ft_send=dma((2,)), ft_recv=dma((n_rep,)), ld_sem=dma((len(LOADED),)), g_send=dma((4,)), g_recv=dma((20,)),
     )
     for key, (_, count) in in_pieces(rows_in).items():
         packed = count * full + count // 2
         scratch["p_" + key] = vm((packed, 128), f32)
         for name in ("s2_", "r2_"):
             scratch[name + key] = vm((4, packed, 128), bf16)
-        scratch["r3_" + key] = vm((n_rep, packed if key == "c" else packed // n_rep, 128), bf16)
-        if key != "c":
+        if key == "c":
+            for name in ("r3_", "r4_"):
+                scratch[name + key] = vm((2, packed, 128), bf16)
+            scratch["r4s_" + key], scratch["r4r_" + key] = dma, dma
+        else:
+            scratch["r3_" + key] = vm((n_rep, packed // n_rep, 128), bf16)
             scratch["pb_" + key] = vm((n_rep, packed // n_rep, 128), bf16)
         for name in ("r2", "r3"):
             scratch[name + "s_" + key], scratch[name + "r_" + key] = dma, dma
@@ -777,7 +846,7 @@
     scratch["tz_v"] = vm((4, packed_out // n_rep, 128), f32)
     for name in ("tzb_v", "r2z_v"):
         scratch[name] = vm((4, packed_out // n_rep, 128), bf16)
-    for key in ("tf", "e", "sm", "ft", "em", "rs", "c0", "c1", "c2", "rz", "r2z"):
+    for key in ("tf", "e", "sm", "em", "c0", "c1", "c2", "rz", "r2z"):
         scratch[key + "_send"], scratch[key + "_recv"] = dma, dma
     shape = jax.ShapeDtypeStruct
     results = dict(

time: 41.9 us -> 41.9 us (level)
  no operation moved by 1% of the time
where the time goes in v4:
time: 41.9 us; the launch traced here: 41.7 us
  Pallas kernels  41 us (98%)
  between operations  0.66 us (2%)
    pallas_call x1, Pallas kernels, fused_device(): pl.pallas_call(functools.partial(fused_kernel, n_rep, n_sam, names), out_...  40 us
    pallas_call x1, Pallas kernels, fused_device(): pl.pallas_call(output_kernel, out_shape=(*big, *flat, *big, *flat), in_sp...  1.03 us

profile of v4, /device:TPU:0, one launch (start us, length us, event | category | flops | bytes accessed | tf_op | source)
XLA Modules:
  0.0 41.7 jit_solution(5423329858974010473)
XLA Ops:
  0.6 40.0 %distill_step.1 = (f32[320,320]{1,0:T(8,128)S(1)}, f32[320,320]{1,0:T(8,128)S(1)}, f32[320]{0:T(512)S(1)}, f32[320]{0:T(512)S(1)}, f32[320]{0:T(512)S(1)}, /*index=5*/f32[320]{0:T(512)S(1)}) custom-call(s32[2]{0:T(128)} %refs_0_.1, f32[160,320]{1,0:T(8,128)} %refs_1_.1, f32[80,320]{1,0:T(8,128)} %refs_2_.1, f32[80,320]{1,0:T(8,128)} %refs_3_.1, ...), custom_call_target="tpu_custom_call" | custom-call | tf_op jit(solution)/shard_map/distill_step/pallas_call | solution.py:861
  40.7 1.0 %output_step.1 = (f32[160,320]{1,0:T(8,128)}, f32[80,320]{1,0:T(8,128)}, f32[80,320]{1,0:T(8,128)}, f32[320]{0:T(512)}, f32[320]{0:T(512)}, /*index=5*/f32[160,3...) custom-call(f32[320,320]{1,0:T(8,128)S(1)} %get-tuple-element.16.grads, ...), custom_call_target="tpu_custom_call" | custom-call | tf_op jit(solution)/shard_map/output_step/pallas_call | solution.py:875

commit v5 on v4

--- a/solution.py
+++ b/solution.py
@@ -202,6 +202,11 @@
     return {"a": (0, big), "b": (big, big), "c": (2 * big, rows - 2 * big)}
 
 
+def out_pieces(rows):
+    big = rows * 3 // 5 // 16 * 16
+    return {"o": (0, big), "d": (big, rows - big)}
+
+
 def fused_kernel(n_rep, n_sam, names, *refs):
     r = dict(zip(names, refs))
     f32, bf16 = jnp.float32, jnp.bfloat16
@@ -210,7 +215,8 @@
     sw, so, st, tw, to, tt = (r[k] for k in ("sw", "so", "st", "tw", "to", "tt"))
     sg, sb, tg, tb, x_s, x_t = (r[k] for k in ("sg", "sb", "tg", "tb", "x_s", "x_t"))
     rows_in, rows_out, rows_time = sw.shape[0], so.shape[0], st.shape[0]
-    pieces = in_pieces(rows_in)
+    pieces = {**in_pieces(rows_in), **out_pieces(rows_out)}
+    first_rows = pieces["o"][1]
     width, tokens = x_s.shape
     per = tokens // n_sam
     lo = width // 128 * 128
@@ -524,8 +530,9 @@
     def pair(key, rel):
         first, count = pieces[key]
         owner = peer(rel)
-        own = r["gs_i"][pl.ds(pl.multiple_of(owner * rows_in + first, 16), count), :]
-        return own + r1_i[lax.div(owner, 2), first : first + count, :].astype(f32)
+        g, r1, stride = (r["gs_o"], r1_o, rows_out) if key == "d" else (r["gs_i"], r1_i, rows_in)
+        own = g[pl.ds(pl.multiple_of(owner * stride + first, 16), count), :]
+        return own + r1[lax.div(owner, 2), first : first + count, :].astype(f32)
 
     def to_chip(key, k):
         s2, r2 = r["s2_" + key], r["r2_" + key]
@@ -575,13 +582,15 @@
     pk_v, z_v, zb_v, rz_v = r["pk_v"], r["z_v"], r["zb_v"], r["rz_v"]
     share = pk_v.shape[0] // n_rep
     for q in range(4):
-        own = r["gs_o"][pl.ds(pl.multiple_of((2 * q + core) * rows_out, 16), rows_out), :]
-        put_packed(pk_v, own + r1_o[q].astype(f32))
+        own = r["gs_o"][pl.ds(pl.multiple_of((2 * q + core) * rows_out, 16), first_rows), :]
+        put_packed(pk_v, own + r1_o[q, :first_rows, :].astype(f32))
         for j in range(n_rep):
             z_v[j, q * share : (q + 1) * share, :] = pk_v[j * share : (j + 1) * share, :]
     for j in range(n_rep):
         zb_v[j] = z_v[j].astype(bf16)
     exchange("rz", lambda j: zb_v.at[rep_peer(j)], lambda j: rz_v.at[j], far, rep_id)
+    for k in (3, 2, 1):
+        to_chip("d", k)
     weight_grad(1)
     arrive(r1_i.at[pl.ds(0, 2)], r["c1_recv"])
     to_chip("a", 3)
@@ -603,7 +612,7 @@
     exchange("sm", lambda t: small.at[me], lambda t: small.at[me], near, dp_id)
     for k in (3, 2, 1):
         to_chip("c", k)
-    for key in "abc":
+    for key in "dabc":
         put_packed(r["p_" + key], pair(key, 0))
 
     def chips_total(key):
@@ -619,6 +628,12 @@
             pb[q] = p[q * part : (q + 1) * part, :].astype(bf16)
         for j in far:
             send(pb.at[rep_peer(j)], r3.at[j], r["r3s_" + key], r["r3r_" + key], rep_id(j))
+
+    def to_planes_whole(key):
+        r3 = r["r3_" + key]
+        r3[pl.ds(rep, 1)] = chips_total(key)[...].astype(bf16)[None]
+        for j in far:
+            send(r3.at[rep], r3.at[rep], r["r3s_" + key], r["r3r_" + key], rep_id(j))
 
     def to_next_plane(key):
         r3 = r["r3_" + key]
@@ -683,15 +698,25 @@
             p[q * part : (q + 1) * part, :] = fin[q].astype(f32)
         finish(start, unpacked(p[...], count, width))
 
+    def collect_direct(key, start):
+        r3 = r["r3_" + key]
+        arrive(r3.at[pl.ds(0, 3)], r["r3r_" + key])
+        total = r3[0].astype(f32)
+        for j in range(1, n_rep):
+            total = total + r3[j].astype(f32)
+        first, count = pieces[key]
+        finish(start + first, unpacked(total, count, width))
+
     def collect_whole(key):
         r4 = r["r4_" + key]
         arrive(r4.at[0], r["r4r_" + key])
         first, count = pieces[key]
         finish(first, unpacked(r4[0].astype(f32) + r4[1].astype(f32), count, width))
 
+    to_planes_whole("d")
     to_planes("a")
+    plane_total()
     to_planes("b")
-    plane_total()
     arrive(small.at[pl.ds(0, 7)], r["sm_recv"])
     part = [small[d].astype(f32) for d in range(8)]
     sums = part[0]
@@ -717,11 +742,12 @@
 
     to_next_plane("c")
     share_total("a")
+    chip_total()
+    collect_direct("d", rows_in)
     share_total("b")
     to_far_plane("c")
-    chip_total()
     pl.when(core == 1)(pass_to_core)
-    collect_whole("c")
+    collect("a", *pieces["a"])
 
     @pl.when(core == 0)
     def _():
@@ -740,13 +766,13 @@
     r["gg_o"][...], r["gb_o_"][...] = gg, gb
     r["eg_o"][...] = average(tg[...], sg[...], gg)
     r["eb_o"][...] = average(tb[...], sb[...], gb)
-    collect("a", *pieces["a"])
+    collect("o", rows_in, first_rows)
     collect("b", *pieces["b"])
-    collect("o", rows_in, rows_out)
+    collect_whole("c")
     for key, ref in (("tf", tf_all), ("e", e_in), ("sm", small)):
         sent.append((ref.at[pl.ds(0, 7)], r[key + "_send"]))
     sent += [(r1_o, r["c0_send"]), (r1_i.at[pl.ds(0, 2)], r["c1_send"]), (r1_i.at[pl.ds(0, 2)], r["c2_send"])]
-    for key in "abc":
+    for key in "abcd":
         sent.append((r["r2_" + key].at[pl.ds(0, 3)], r["r2s_" + key]))
         sent.append((r["r3_" + key].at[0] if key == "c" else r["r3_" + key].at[pl.ds(0, 3)], r["r3s_" + key]))
     sent.append((r["r4_c"].at[0], r["r4s_c"]))
@@ -798,7 +824,9 @@
     full = width // 128
     rows_emb = -(-(2 * n_sam * full + n_sam) // SUB) * SUB
     rows_small = -(-((n_sam + 4) * full + (n_sam + 4) // 2) // 16) * 16
-    packed_in, packed_out = rows_in * full + rows_in // 2, rows_out * full + rows_out // 2
+    packed_in = rows_in * full + rows_in // 2
+    first_rows = out_pieces(rows_out)["o"][1]
+    packed_out = first_rows * full + first_rows // 2
     scratch = dict(
         ts=pltpu.SMEM((n_sam,), jnp.int32),
         sw=vm(sw.shape, f32), so=vm(so.shape, f32), st=vm(st.shape, f32),
@@ -822,7 +850,7 @@
         r1_i=vm((4, rows_in, width), bf16), r1_o=vm((4, rows_out, width), bf16),
         rs_send=dma, ft_send=dma((2,)), ft_recv=dma((n_rep,)), ld_sem=dma((len(LOADED),)), g_send=dma((4,)), g_recv=dma((20,)),
     )
-    for key, (_, count) in in_pieces(rows_in).items():
+    for key, (_, count) in (*in_pieces(rows_in).items(), ("d", out_pieces(rows_out)["d"])):
         packed = count * full + count // 2
         scratch["p_" + key] = vm((packed, 128), f32)
         for name in ("s2_", "r2_"):
@@ -831,6 +859,8 @@
             for name in ("r3_", "r4_"):
                 scratch[name + key] = vm((2, packed, 128), bf16)
             scratch["r4s_" + key], scratch["r4r_" + key] = dma, dma
+        elif key == "d":
+            scratch["r3_" + key] = vm((n_rep, packed, 128), bf16)
         else:
             scratch["r3_" + key] = vm((n_rep, packed // n_rep, 128), bf16)
             scratch["pb_" + key] = vm((n_rep, packed // n_rep, 128), bf16)
@@ -900,6 +930,7 @@
         and all(r % (32 * n_dp) == 0 for r in rows[:1])
         and in_pieces(rows[0] // n_dp)["a"][1] % 64 == 0
         and in_pieces(rows[0] // n_dp)["a"][1] > 0
+        and out_pieces(rows[1] // n_dp)["o"][1] > 0
         and rows[0] == 2 * rows[1]
         and rows[2] == rows[1]
         and args[0].shape[1] % 128 == 64

time: 41.9 us -> 41.1 us (0.981)
  Pallas kernels: 41 us -> 40.3 us
    pallas_call x1, Pallas kernels: 40 us -> 39.3 us  [fused_device(): pl.pallas_call(functools.partial(fused_kernel, n_rep, n_sam, names), out_...]
where the time goes in v5:
time: 41.1 us; the launch traced here: 41 us
  Pallas kernels  40.3 us (98%)
  between operations  0.66 us (2%)
    pallas_call x1, Pallas kernels, fused_device(): pl.pallas_call(functools.partial(fused_kernel, n_rep, n_sam, names), out_...  39.3 us
    pallas_call x1, Pallas kernels, fused_device(): pl.pallas_call(output_kernel, out_shape=(*big, *flat, *big, *flat), in_sp...  1.03 us

profile of v5, /device:TPU:0, one launch (start us, length us, event | category | flops | bytes accessed | tf_op | source)
XLA Modules:
  0.0 41.0 jit_solution(1229078209285173869)
XLA Ops:
  0.6 39.3 %distill_step.1 = (f32[320,320]{1,0:T(8,128)S(1)}, f32[320,320]{1,0:T(8,128)S(1)}, f32[320]{0:T(512)S(1)}, f32[320]{0:T(512)S(1)}, f32[320]{0:T(512)S(1)}, /*index=5*/f32[320]{0:T(512)S(1)}) custom-call(s32[2]{0:T(128)} %refs_0_.1, f32[160,320]{1,0:T(8,128)} %refs_1_.1, f32[80,320]{1,0:T(8,128)} %refs_2_.1, f32[80,320]{1,0:T(8,128)} %refs_3_.1, ...), custom_call_target="tpu_custom_call" | custom-call | tf_op jit(solution)/shard_map/distill_step/pallas_call | solution.py:891
  39.9 1.0 %output_step.1 = (f32[160,320]{1,0:T(8,128)}, f32[80,320]{1,0:T(8,128)}, f32[80,320]{1,0:T(8,128)}, f32[320]{0:T(512)}, f32[320]{0:T(512)}, /*index=5*/f32[160,3...) custom-call(f32[320,320]{1,0:T(8,128)S(1)} %get-tuple-element.16.grads, ...), custom_call_target="tpu_custom_call" | custom-call | tf_op jit(solution)/shard_map/output_step/pallas_call | solution.py:905

commit v6 on v5

--- a/solution.py
+++ b/solution.py
@@ -275,16 +275,18 @@
     def arrive(ref, sem):
         bytes_of(ref, sem).wait_recv()
 
+    for name in PACKED_SENDS:
+        r[name] = r["g_s"]
     sent = []
 
     def exchange(key, source, slots, peers, where):
         for j in peers:
             src, dst = source(j), slots(j)
-            send(src, dst, r[key + "_send"], r[key + "_recv"], where(j))
+            send(src, dst, r[key + "_s"], r[key + "_r"], where(j))
 
     bufs = (r["p_sin"], r["p_out"], r["p_tin"], r["p_tout"])
     s_in, out, t_in, t_out = range(4)
-    g_send, g_recv = r["g_send"], r["g_recv"]
+    g_s, g_r = r["g_s"], r["g_r"]
     loaded("ts")
     line = lax.broadcasted_iota(jnp.int32, (SUB, rows_time), 0)
     lane = lax.broadcasted_iota(jnp.int32, (SUB, rows_time), 1)
@@ -310,23 +312,27 @@
     def push(seg, orel, t, r_at, start=0, count=None):
         count = bufs[seg].shape[1] if count is None else count
         part = bufs[seg].at[peer(orel), pl.ds(start, count)]
-        send(part, part, g_send.at[seg], g_recv.at[seg * 5 + r_at], dp_id(t))
+        send(part, part, g_s, g_r.at[seg * 5 + r_at], dp_id(t))
 
     def landed(seg, r_at, count=1):
-        arrive(bufs[seg].at[pl.ds(0, count)], g_recv.at[seg * 5 + r_at])
+        arrive(bufs[seg].at[pl.ds(0, count)], g_r.at[seg * 5 + r_at])
 
     def landed_rows(seg, r_at, count):
-        arrive(bufs[seg].at[0, pl.ds(0, count)], g_recv.at[seg * 5 + r_at])
+        arrive(bufs[seg].at[0, pl.ds(0, count)], g_r.at[seg * 5 + r_at])
 
     def open_gather(seg):
         c = cut(seg)
         d = bufs[seg].shape[1] - c
         push(seg, 0, 2, 0, 0, c)
         push(seg, 0, 4, 1, c, d)
-        push(seg, 0, 2, 4, c, d)
+        if seg != t_in:
+            open_rest(seg)
+        push(seg, 0, 1, 3)
+
+    def open_rest(seg):
+        c = cut(seg)
+        push(seg, 0, 2, 4, c, bufs[seg].shape[1] - c)
         push(seg, 0, 4, 4, 0, c)
-        push(seg, 0, 1, 3)
-        sent.append((bufs[seg].at[pl.ds(0, 7)], g_send.at[seg]))
 
     def relay(seg):
         c = cut(seg)
@@ -385,7 +391,7 @@
     bufs[out][me, at, :] = jnp.concatenate([so[:, lo:], to[:, lo:]], axis=1).astype(bf16)
     loaded("st", "tt")
     st_b, tt_b = st[...].astype(bf16), tt[...].astype(bf16)
-    arrive(tf_all.at[pl.ds(0, 7)], r["tf_recv"])
+    arrive(tf_all.at[pl.ds(0, 7)], r["tf_r"])
     feats = tf_all[...].reshape(8 * SUB, rows_time).astype(bf16)
     part_s = jnp.dot(feats, st_b, preferred_element_type=f32)
     part_t = jnp.dot(feats, tt_b, preferred_element_type=f32)
@@ -396,6 +402,7 @@
     e_in[pl.ds(me, 1)] = e_part[pl.ds(me, 1)]
     exchange("e", lambda t: e_part.at[peer(t)], lambda t: e_in.at[me], near, dp_id)
     relay(s_in)
+    open_rest(t_in)
     open_gather(out)
     open_gather(t_out)
 
@@ -411,11 +418,11 @@
                 b = rep + back * hops
                 at = ft_all.at[b]
                 if hops:
-                    arrive(at, r["ft_recv"].at[b])
+                    arrive(at, r["ft_r"].at[b])
 
                 @pl.when(onward)
                 def _():
-                    send(at, at, r["ft_send"].at[(1 + back) // 2], r["ft_recv"].at[b], {"rep": rep - back})
+                    send(at, at, r["ft_s"].at[(1 + back) // 2], r["ft_r"].at[b], {"rep": rep - back})
 
     def features_sent():
         for k in range(n_rep):
@@ -423,9 +430,9 @@
             @pl.when(rep == k)
             def _(k=k):
                 if k < n_rep - 1:
-                    bytes_of(ft_all.at[pl.ds(0, k + 1)], r["ft_send"].at[0]).wait_send()
+                    bytes_of(ft_all.at[pl.ds(0, k + 1)], r["ft_s"].at[0]).wait_send()
                 if k > 0:
-                    bytes_of(ft_all.at[pl.ds(0, n_rep - k)], r["ft_send"].at[1]).wait_send()
+                    bytes_of(ft_all.at[pl.ds(0, n_rep - k)], r["ft_s"].at[1]).wait_send()
 
     pass_features(0)
     start = 0
@@ -444,7 +451,7 @@
     for k in range(n_sam):
         xt_v[pl.ds(k * per, per), :] = x_t[:, pl.ds(k * per, per)].astype(f32).T
 
-    arrive(e_in.at[pl.ds(0, 7)], r["e_recv"])
+    arrive(e_in.at[pl.ds(0, 7)], r["e_r"])
     emb = e_in[0]
     for k in range(1, 8):
         emb = emb + e_in[k]
@@ -525,7 +532,7 @@
 
     def to_core(src, dst, count, q, key):
         part = src.at[pl.ds(pl.multiple_of((2 * q + 1 - core) * count, 16), count)]
-        send(part, dst.at[q], r[key + "_send"], r[key + "_recv"], dp_id(1))
+        send(part, dst.at[q], r[key + "_s"], r[key + "_r"], dp_id(1))
 
     def pair(key, rel):
         first, count = pieces[key]
@@ -578,7 +585,7 @@
         return jnp.sum(gz * normed, axis=0, keepdims=True), jnp.sum(gz, axis=0, keepdims=True)
 
     weight_grad(0)
-    arrive(r1_o, r["c0_recv"])
+    arrive(r1_o, r["c0_r"])
     pk_v, z_v, zb_v, rz_v = r["pk_v"], r["z_v"], r["zb_v"], r["rz_v"]
     share = pk_v.shape[0] // n_rep
     for q in range(4):
@@ -592,14 +599,14 @@
     for k in (3, 2, 1):
         to_chip("d", k)
     weight_grad(1)
-    arrive(r1_i.at[pl.ds(0, 2)], r["c1_recv"])
+    arrive(r1_i.at[pl.ds(0, 2)], r["c1_r"])
     to_chip("a", 3)
     to_chip("a", 2)
     for k in range(n_sam):
         more_gain, more_bias = input_grad(k)
         grad_gain, grad_bias = grad_gain + more_gain, grad_bias + more_bias
         if k == 0:
-            arrive(r1_i.at[pl.ds(0, 2)], r["c2_recv"])
+            arrive(r1_i.at[pl.ds(0, 2)], r["c2_r"])
             to_chip("a", 1)
             for q in (3, 2, 1):
                 to_chip("b", q)
@@ -649,7 +656,7 @@
         send(r4.at[slot], r4.at[slot], r["r4s_" + key], r["r4r_" + key], rep_id(2))
 
     def plane_total():
-        arrive(rz_v.at[pl.ds(1, 3)], r["rz_recv"])
+        arrive(rz_v.at[pl.ds(1, 3)], r["rz_r"])
         tz_v, tzb_v = r["tz_v"], r["tzb_v"]
         total = z_v[rep]
         for j in range(1, n_rep):
@@ -664,7 +671,7 @@
         )
 
     def chip_total():
-        arrive(r["r2z_v"].at[pl.ds(1, 3)], r["r2z_recv"])
+        arrive(r["r2z_v"].at[pl.ds(1, 3)], r["r2z_r"])
         total = r["tz_v"][lax.div(me, 2)]
         for k in (1, 2, 3):
             total = total + r["r2z_v"][k].astype(f32)
@@ -717,7 +724,7 @@
     to_planes("a")
     plane_total()
     to_planes("b")
-    arrive(small.at[pl.ds(0, 7)], r["sm_recv"])
+    arrive(small.at[pl.ds(0, 7)], r["sm_r"])
     part = [small[d].astype(f32) for d in range(8)]
     sums = part[0]
     for k in range(1, 8):
@@ -735,10 +742,10 @@
         exchange("em", lambda j: em_all.at[rep], lambda j: em_all.at[rep], far, rep_id)
 
     def pass_to_core():
-        arrive(em_all.at[pl.ds(0, 3)], r["em_recv"])
+        arrive(em_all.at[pl.ds(0, 3)], r["em_r"])
         for j in far:
             at = em_all.at[rep_peer(j)]
-            send(at, at, r["rs_send"], r["em_recv"], dp_id(1))
+            send(at, at, r["rs_s"], r["em_r"], dp_id(1))
 
     to_next_plane("c")
     share_total("a")
@@ -751,7 +758,7 @@
 
     @pl.when(core == 0)
     def _():
-        arrive(em_all.at[pl.ds(0, 3)], r["em_recv"])
+        arrive(em_all.at[pl.ds(0, 3)], r["em_r"])
 
     grad_time = jnp.zeros((rows_time, width), f32)
     for j in range(n_rep):
@@ -769,26 +776,22 @@
     collect("o", rows_in, first_rows)
     collect("b", *pieces["b"])
     collect_whole("c")
-    for key, ref in (("tf", tf_all), ("e", e_in), ("sm", small)):
-        sent.append((ref.at[pl.ds(0, 7)], r[key + "_send"]))
-    sent += [(r1_o, r["c0_send"]), (r1_i.at[pl.ds(0, 2)], r["c1_send"]), (r1_i.at[pl.ds(0, 2)], r["c2_send"])]
-    for key in "abcd":
-        sent.append((r["r2_" + key].at[pl.ds(0, 3)], r["r2s_" + key]))
-        sent.append((r["r3_" + key].at[0] if key == "c" else r["r3_" + key].at[pl.ds(0, 3)], r["r3s_" + key]))
-    sent.append((r["r4_c"].at[0], r["r4s_c"]))
-    sent += [(rz_v.at[pl.ds(0, 3)], r["rz_send"]), (r["r2z_v"].at[pl.ds(0, 3)], r["r2z_send"])]
-    for key in "oab":
-        sent.append((r["fin_" + key].at[pl.ds(0, 3)], r["r4s_" + key]))
+    sent.append((r["all_v"], g_s))
+    for key, ref in (("tf", tf_all), ("e", e_in)):
+        sent.append((ref.at[pl.ds(0, 7)], r[key + "_s"]))
+    sent += [(r1_o, r["c0_s"]), (r1_i.at[pl.ds(0, 2)], r["c1_s"]), (r1_i.at[pl.ds(0, 2)], r["c2_s"])]
+    sent += [(r["r2z_v"].at[pl.ds(0, 3)], r["r2z_s"]), (r["fin_o"].at[pl.ds(0, 3)], r["r4s_o"])]
     for ref, sem in sent:
         bytes_of(ref, sem).wait_send()
     features_sent()
 
     @pl.when(core == 1)
     def _():
-        for key in ("em_send", "rs_send"):
+        for key in ("em_s", "rs_s"):
             bytes_of(em_all.at[pl.ds(0, 3)], r[key]).wait_send()
 
 
+PACKED_SENDS = ("sm_s", "rz_s", "r4s_a", "r4s_b", "r4s_c") + tuple(n + k for n in ("r2s_", "r3s_") for k in "abcd")
 LOADED = ("ts", "sw", "so", "to", "tw", "st", "tt", "x_s", "sg", "sb", "x_t", "tg", "tb")
 
 
@@ -848,7 +851,7 @@
         gs_i=vm((n_dp * rows_in, width), f32), gs_o=vm((ff, width), f32),
         gb_i=vm((n_dp * rows_in, width), bf16), gb_o=vm((ff, width), bf16),
         r1_i=vm((4, rows_in, width), bf16), r1_o=vm((4, rows_out, width), bf16),
-        rs_send=dma, ft_send=dma((2,)), ft_recv=dma((n_rep,)), ld_sem=dma((len(LOADED),)), g_send=dma((4,)), g_recv=dma((20,)),
+        rs_s=dma, ft_s=dma((2,)), ft_r=dma((n_rep,)), ld_sem=dma((len(LOADED),)), g_s=dma, g_r=dma((20,)),
     )
     for key, (_, count) in (*in_pieces(rows_in).items(), ("d", out_pieces(rows_out)["d"])):
         packed = count * full + count // 2
@@ -877,7 +880,15 @@
     for name in ("tzb_v", "r2z_v"):
         scratch[name] = vm((4, packed_out // n_rep, 128), bf16)
     for key in ("tf", "e", "sm", "em", "c0", "c1", "c2", "rz", "r2z"):
-        scratch[key + "_send"], scratch[key + "_recv"] = dma, dma
+        scratch[key + "_s"], scratch[key + "_r"] = dma, dma
+    whole = packed_in * 2 + rows_out * (2 * full + 1)
+    rows_sent = 7 * (whole + rows_small) + 3 * packed_out
+    for key in "abcd":
+        packed = scratch["p_" + key].shape[0]
+        rows_sent += 3 * packed + {"a": 6 * packed // n_rep, "b": 6 * packed // n_rep, "c": 2 * packed, "d": 3 * packed}[key]
+    scratch["all_v"] = vm((rows_sent, 128), bf16)
+    for name in PACKED_SENDS:
+        scratch.pop(name, None)
     shape = jax.ShapeDtypeStruct
     results = dict(
         g_o=shape((rows_all, width), f32), e_o=shape((rows_all, width), f32), gg_o=shape((width,), f32),

time: 41.1 us -> 41 us (level)
  no operation moved by 1% of the time
where the time goes in v6:
time: 41 us; the launch traced here: 40.8 us
  Pallas kernels  40.1 us (98%)
  between operations  0.66 us (2%)
    pallas_call x1, Pallas kernels, fused_device(): pl.pallas_call(functools.partial(fused_kernel, n_rep, n_sam, names), out_...  39.1 us
    pallas_call x1, Pallas kernels, fused_device(): pl.pallas_call(output_kernel, out_shape=(*big, *flat, *big, *flat), in_sp...  1.03 us

profile of v6, /device:TPU:0, one launch (start us, length us, event | category | flops | bytes accessed | tf_op | source)
XLA Modules:
  0.0 40.8 jit_solution(11401832215473047876)
XLA Ops:
  0.6 39.1 %distill_step.1 = (f32[320,320]{1,0:T(8,128)S(1)}, f32[320,320]{1,0:T(8,128)S(1)}, f32[320]{0:T(512)S(1)}, f32[320]{0:T(512)S(1)}, f32[320]{0:T(512)S(1)}, /*index=5*/f32[320]{0:T(512)S(1)}) custom-call(s32[2]{0:T(128)} %refs_0_.1, f32[160,320]{1,0:T(8,128)} %refs_1_.1, f32[80,320]{1,0:T(8,128)} %refs_2_.1, f32[80,320]{1,0:T(8,128)} %refs_3_.1, ...), custom_call_target="tpu_custom_call" | custom-call | tf_op jit(solution)/shard_map/distill_step/pallas_call | solution.py:902
  39.8 1.0 %output_step.1 = (f32[160,320]{1,0:T(8,128)}, f32[80,320]{1,0:T(8,128)}, f32[80,320]{1,0:T(8,128)}, f32[320]{0:T(512)}, f32[320]{0:T(512)}, /*index=5*/f32[160,3...) custom-call(f32[320,320]{1,0:T(8,128)S(1)} %get-tuple-element.16.grads, ...), custom_call_target="tpu_custom_call" | custom-call | tf_op jit(solution)/shard_map/output_step/pallas_call | solution.py:916
